TPU v7x, 32 devices: a whole 2x2x4 slice. The times are simulated.
32 devices in a mesh: lat: 4 (over y, x), lon: 4 (over z), ens: 2 (over core).
Axes of the slice: x: 2, y: 2, z: 4, core: 2. Of those that a mesh axis runs over, the one named last changes fastest.
Arguments:
- parameters: float32 [2, 128, 32, 512], P(None, 'ens', 'lat', 'lon'), may hold values from -1.2 to 1.2, as said below
- initial_height: float32 [32, 512], P('lat', 'lon'), may hold values from -6 to 6
- initial_speed: float32 [2, 32, 512], P(None, 'lat', 'lon'), may hold values from -4 to 4
- obs_slots: int32 [2, 16, 16, 8], P(None, ('lat', 'lon')), may hold values from -1 to 1023, as said below
- obs_values: float32 [2, 16, 16, 8], P(None, ('lat', 'lon')), may hold values from -6 to 6
- obs_precision: float32 [2, 16, 16, 8], P(None, ('lat', 'lon')), may hold values from 0 to 2, as said below
Outputs:
- calibrated: float32 [2, 128, 32, 512], P(None, 'ens', 'lat', 'lon')
Inputs may be any that keep to these rules, and one draw needn't show every extreme that they name: `obs_slots`: for each iteration and owner, the live slots towards one receiver come first and name distinct cells of the owner's block (local index row * 128 + column); no cell is named twice by one owner in one iteration; in each iteration some receiving block has all 8 slots live from every owner. `obs_precision`: zero exactly where the matching slot of obs_slots (with receiver and owner swapped) is empty, 0.5 or more elsewhere. `parameters`: friction rates lie in 0.02 to 0.2, forcing in -1.2 to 1.2.
All inputs are finite; a program needn't handle non-finite values.
Results may differ from a plain program's by a relative error of at most 0.0003.
Values sent between devices are 32-bit elements; how exact they have to be, the bound alone decides.
A program may use at most 64 MiB of HBM per device.

v0:
```python
import math

import functools

import jax
import jax.numpy as jnp
from jax import lax
from jax.experimental import pallas as pl
from jax.experimental.pallas import tpu as pltpu
from jax.sharding import PartitionSpec as P

STEPS = 6
ITERS = 2


depth_step = 0.7
gravity_step = 0.7
coriolis = 0.1


def padded_2(value, sides, width, wrap):
    for axis, dim in sides:
        peers, length = (lax.axis_size(axis), value.shape[dim])
        up = [(i, (i + 1) % peers) for i in range(peers if wrap else peers - 1)]
        down = [(j, i) for i, j in up]
        last = lax.slice_in_dim(value, length - width, length, axis=dim)
        leading = lax.slice_in_dim(value, 0, width, axis=dim)
        before = lax.ppermute(last, axis, up)
        after = lax.ppermute(leading, axis, down)
        value = jnp.concatenate([before, value, after], axis=dim)
    return value


def wall_rows(padded):
    row_count = padded.shape[-2]
    position = lax.axis_index("lat")
    last_block = lax.axis_size("lat") - 1
    row_ids = lax.broadcasted_iota(jnp.int32, (row_count, 1), 0)
    lower_wall = jnp.logical_and(row_ids == 0, position == 0)
    upper_wall = jnp.logical_and(row_ids == row_count - 1, position == last_block)
    keep_rows = jnp.logical_not(jnp.logical_or(lower_wall, upper_wall))
    return padded * keep_rows.astype(padded.dtype)


def advance(height, speeds, friction, forcing):
    east_padded = padded_2(speeds[0], (("lon", 2),), 1, True)
    north_padded = padded_2(speeds[1], (("lat", 1),), 1, False)
    east_diff = east_padded[:, :, 2:] - east_padded[:, :, :-2]
    north_diff = north_padded[:, 2:, :] - north_padded[:, :-2, :]
    height = height - depth_step * (east_diff + north_diff) + forcing
    padded_height = padded_2(height, (("lat", 1), ("lon", 2)), 1, True)
    padded_height = wall_rows(padded_height)
    slope_east = padded_height[:, 1:-1, 2:] - padded_height[:, 1:-1, :-2]
    slope_north = padded_height[:, 2:, 1:-1] - padded_height[:, :-2, 1:-1]
    eastward = (1.0 - friction) * speeds[0] - gravity_step * slope_east + coriolis * speeds[1]
    northward = (1.0 - friction) * speeds[1] - gravity_step * slope_north - coriolis * speeds[0]
    return (height, jnp.stack([eastward, northward]))


def forward(parameters, initial_height, initial_speed):
    members = parameters.shape[1]
    height = jnp.broadcast_to(initial_height, (members,) + initial_height.shape)
    speeds = jnp.broadcast_to(initial_speed[:, None], (2, members) + initial_height.shape)
    for substep in range(STEPS):
        height, speeds = advance(height, speeds, parameters[0], parameters[1])
    return height


def predict(height, cells):
    flattened = height.reshape(height.shape[0], -1)
    wanted = cells.reshape(-1)
    picked = jnp.take(flattened, jnp.clip(wanted, 0, flattened.shape[1] - 1), axis=1)
    picked = jnp.where(wanted[None, :] >= 0, picked, jnp.float32(0.0))
    return picked.T.reshape(cells.shape[0], -1)


def gram_terms(predicted, observed, precision):
    members = predicted.shape[1]
    centre = jnp.mean(predicted, axis=1, keepdims=True)
    spread = predicted - centre
    weighted = spread * precision[:, None]
    misfit = observed[:, None] - predicted
    gram_part = jnp.dot(spread.T, weighted, precision=lax.Precision.HIGHEST) / members
    cross_part = jnp.dot(weighted.T, misfit, precision=lax.Precision.HIGHEST) / math.sqrt(members)
    return (gram_part, cross_part)


def solve_weights(gram_part, cross_part):
    members = gram_part.shape[0]
    system = jnp.eye(members, dtype=jnp.float32) + gram_part
    factor = jnp.linalg.cholesky(system)
    weights = jax.scipy.linalg.cho_solve((factor, True), cross_part) / math.sqrt(members)
    return weights - jnp.mean(weights, axis=0, keepdims=True)


def per_device_halo(parameters, initial_height, initial_speed, obs_slots, obs_values, obs_precision):
    owners = obs_slots.shape[2]
    slot_count = obs_slots.shape[3]
    members_here = parameters.shape[1]
    member_block = lax.axis_index("ens")
    owner_values, owner_precision = (
        lax.all_to_all(obs_values[:, 0], ("lat", "lon"), split_axis=1, concat_axis=1, tiled=True),
        lax.all_to_all(
            obs_precision[:, 0], ("lat", "lon"), split_axis=1, concat_axis=1, tiled=True
        ),
    )
    for iteration in range(ITERS):
        height = forward(parameters, initial_height, initial_speed)
        outgoing = predict(height, obs_slots[iteration, 0])
        received = outgoing
        observed = owner_values[iteration]
        precision = owner_precision[iteration]
        received = received.reshape(owners, slot_count, members_here)
        gathered = lax.all_gather(received, "ens", axis=2, tiled=True)
        members = gathered.shape[2]
        gram_part, cross_part = gram_terms(
            gathered.reshape(-1, members), observed.reshape(-1), precision.reshape(-1)
        )
        gram_part, cross_part = lax.psum((gram_part, cross_part), ("lat", "lon"))
        centred = solve_weights(gram_part, cross_part)
        local_weights = lax.dynamic_slice_in_dim(
            centred, member_block * members_here, members_here, 1
        )
        starting = jnp.zeros(
            (2, members_here, parameters.shape[2] * parameters.shape[3]), jnp.float32
        )
        pieces = lax.all_gather(parameters, "ens", axis=1, tiled=True)
        stacked = pieces.reshape(pieces.shape[0], pieces.shape[1], -1)
        increment = starting + jnp.einsum(
            "pjc,jm->pmc", stacked, local_weights, precision=lax.Precision.HIGHEST
        )
        parameters = parameters + increment.reshape(parameters.shape)
    return parameters


MESH = pl.DeviceIdType.MESH
VMEM = pltpu.VMEM
EDGE = 16
SUB = 8
CHUNK = 4


def east(field):
    width, axis = (field.shape[-1], field.ndim - 1)
    return pltpu.roll(field, width - 1, axis) - pltpu.roll(field, 1, axis)


def north(field, first_row, last_row):
    height = field.shape[0]
    after = jnp.where(last_row, 0.0, pltpu.roll(field, height - 1, 0))
    before = jnp.where(first_row, 0.0, pltpu.roll(field, 1, 0))
    return after - before


def flat_line(block, width):
    depth, count = block.shape
    lanes = lax.broadcasted_iota(jnp.int32, (count, width), 1)
    slots = lax.broadcasted_iota(jnp.int32, (count, width), 0)
    spread_out = jnp.dot(
        block,
        (lax.rem(lanes, count) == slots).astype(jnp.float32),
        precision=lax.Precision.HIGHEST,
        preferred_element_type=jnp.float32,
    )
    owners = lax.broadcasted_iota(jnp.int32, (depth, width), 0)
    groups = lax.broadcasted_iota(jnp.int32, (depth, width), 1) // count
    return jnp.sum(jnp.where(owners == groups, spread_out, 0.0), axis=0, keepdims=True)


def each(start, count, body):
    def step(i, carry):
        body(i)
        return carry

    lax.fori_loop(start, count, step, 0)


def send(src, dst, send_sem, recv_sem, device):
    return pltpu.make_async_remote_copy(
        src_ref=src,
        dst_ref=dst,
        send_sem=send_sem,
        recv_sem=recv_sem,
        device_id=device,
        device_id_type=MESH,
    )


def run_group(k, got, start, height, speed_e, speed_n):
    rows = start.shape[1]
    chunks = [pl.ds(c, CHUNK) for c in range(0, rows, CHUNK)]
    upper = [pl.ds(c + 2, CHUNK) for c in range(0, rows, CHUNK)]
    inner = [pl.ds(c + 1, CHUNK) for c in range(0, rows, CHUNK)]

    def new_speeds(n, keep, old_e, old_n):
        slope_e = east(height[inner[n]])
        slope_n = height[upper[n]] - height[chunks[n]]
        speed_e[chunks[n]] = keep * old_e - gravity_step * slope_e + coriolis * old_n
        speed_n[inner[n]] = keep * old_n - gravity_step * slope_n - coriolis * old_e

    def new_height():
        for n in range(len(chunks)):
            flow = east(speed_e[chunks[n]]) + (speed_n[upper[n]] - speed_n[chunks[n]])
            height[inner[n]] = height[inner[n]] - depth_step * flow + got[k, 1, chunks[n]]

    for n in range(len(chunks)):
        height[inner[n]] = start[0, chunks[n]] + got[k, 1, chunks[n]]
    for n in range(len(chunks)):
        keep = 1.0 - got[k, 0, chunks[n]]
        got[k, 0, chunks[n]] = keep
        new_speeds(n, keep, start[1, chunks[n]], start[2, chunks[n]])

    def middle(step, carry):
        new_height()
        for n in range(len(chunks)):
            new_speeds(n, got[k, 0, chunks[n]], speed_e[chunks[n]], speed_n[inner[n]])
        return carry

    lax.fori_loop(1, STEPS - 1, middle, 0)
    new_height()


def ensemble_kernel(iteration, n_lat, n_lon, n_ens, *refs):
    first = iteration == 0
    if first:
        params, start_height, start_speed, slots_in, values_in, precision_in = refs[:6]
        gx, other, own, fields, cells, info = refs[6:12]
        aux, lin, fin, send_a, recv_a, send_l, recv_l = refs[12:19]
        refs = refs[19:]
    else:
        own, fields, cells, info, gx, other = refs[:6]
        refs = refs[6:]
    (got, edges, goth, start, height, speed_e, speed_n) = refs[:7]
    (outgoing, arrived, part, partner_part, half_sum, halves) = refs[7:13]
    (send_p, recv_p, send_h, recv_h, send_o, recv_o) = refs[13:19]
    (send_y, recv_y, send_x, recv_x, send_z, recv_z) = refs[19:]
    lat, lon, ens = (lax.axis_index("lat"), lax.axis_index("lon"), lax.axis_index("ens"))
    blocks = n_lat * n_lon
    me = lat * n_lon + lon
    column = n_lat * n_ens
    here = ens * n_lat + lat
    rows, cols = fields.shape[1] // n_lat, got.shape[-1] // 2
    groups_here = got.shape[0]
    groups = n_lat * groups_here
    share = n_lat // n_ens

    def at(lat_to, lon_to, ens_to):
        return {"lat": lat_to, "lon": lon_to, "ens": ens_to}

    def same_column(flat):
        return at(lax.rem(flat, n_lat), lon, flat // n_lat)

    def same_core(block):
        return at(block // n_lon, lax.rem(block, n_lon), ens)

    def east_of(d):
        return lax.rem(lon + d + n_lon, n_lon)

    barrier = pltpu.get_barrier_semaphore()

    def greet(device):
        pl.semaphore_signal(barrier, inc=1, device_id=device, device_id_type=MESH)

    each(1, blocks, lambda i: greet(same_core(lax.rem(me + i, blocks))))
    each(0, n_lat, lambda i: greet(at(i, lon, 1 - ens)))
    lane = lax.broadcasted_iota(jnp.int32, (SUB, cols), 1)

    if first:
        for g in range(groups):
            for p in range(2):
                for r in range(rows):
                    own[g, p, r] = params[p, g * SUB : (g + 1) * SUB, r, :]
        lines = []
        for ref in (slots_in, values_in, precision_in):
            for t in range(ITERS):
                lines.append(flat_line(ref[t, 0].astype(jnp.float32), cols))
        lines.append(jnp.zeros((rows - len(lines), cols), jnp.float32))
        aux[0] = start_height[...]
        aux[1] = start_speed[0]
        aux[2] = start_speed[1]
        aux[3] = jnp.concatenate(lines, axis=0)

    def pack_edges(g):
        for p in range(2):
            left = jnp.zeros((SUB, cols), jnp.float32)
            right = left
            for r in range(rows):
                tile = own[g, p, r]
                here_lanes = lane // EDGE == r
                left = jnp.where(here_lanes, pltpu.roll(tile, EDGE * r, 1), left)
                shift = (EDGE * r + EDGE) % cols
                right = jnp.where(here_lanes, pltpu.roll(tile, shift, 1), right)
            edges[0, g, p] = left
            edges[1, g, p] = right

    for g in range(groups):
        pack_edges(g)
    zero_row = jnp.zeros((1, SUB, 2 * cols), jnp.float32)
    for ref in (height, speed_n):
        ref[0:1] = zero_row
        ref[ref.shape[0] - 1 : ref.shape[0]] = zero_row
    pl.semaphore_wait(barrier, blocks - 1 + n_lat)

    def field_copy(i, d):
        return send(
            aux.at[0:3],
            fin.at[d % 3, lat],
            send_a.at[i, d % 3],
            recv_a.at[i, d % 3],
            at(lax.rem(lat + i, n_lat), east_of(-d), ens),
        )

    def line_copy(i):
        return send(
            aux.at[3],
            lin.at[me],
            send_l.at[i],
            recv_l.at[i],
            same_core(lax.rem(me + i, blocks)),
        )

    def param_copy(k, i):
        to = lax.rem(lat + i, n_lat)
        return send(
            own.at[to * groups_here + k],
            got.at[k, :, pl.ds(lat * rows, rows), :, pl.ds(0, cols)],
            send_p.at[k, i],
            recv_p.at[k, i],
            at(to, lon, ens),
        )

    def edge_copy(k, i, side):
        to = lax.rem(lat + i, n_lat)
        return send(
            edges.at[side, to * groups_here + k],
            goth.at[k, lat, side],
            send_h.at[k, i, side],
            recv_h.at[k, i, side],
            at(to, east_of(2 * side - 1), ens),
        )

    swap = send(own, other, send_o.at[0], recv_o.at[0], at(lat, lon, 1 - ens))

    if first:
        each(1, n_lat, lambda i: field_copy(i, 0).start())
        for d in (1, -1):
            each(0, n_lat, lambda i: field_copy(i, d).start())
    for k in range(groups_here):
        each(1, n_lat, lambda i: param_copy(k, i).start())
        for side in range(2):
            each(0, n_lat, lambda i: edge_copy(k, i, side).start())
        if first and k == 0:
            each(1, blocks, lambda i: line_copy(i).start())
    swap.start()

    own_rows = pl.ds(lat * rows, rows)
    for k in range(groups_here):
        got[k, :, own_rows, :, 0:cols] = own[lat * groups_here + k]

    if first:
        for i in range(3):
            fin[0, pl.ds(lat, 1), i] = aux[i : i + 1]
        lin[pl.ds(me, 1)] = aux[3:4]
        each(1, n_lat, lambda i: field_copy(i, 0).wait())
        for d in (1, -1):
            each(0, n_lat, lambda i: field_copy(i, d).wait())

        def whole(i):
            lines = []
            for a in range(n_lat):
                after, before = (fin[1, a, i], fin[2, a, i])
                outer = jnp.where(
                    lane < EDGE, after, jnp.where(lane >= cols - EDGE, before, 0.0)
                )
                lines.append(jnp.concatenate([fin[0, a, i], outer], axis=1))
            return jnp.concatenate(lines, axis=0)

        row_ids = lax.broadcasted_iota(jnp.int32, fields.shape[1:], 0)
        first_row, last_row = (row_ids == 0, row_ids == fields.shape[1] - 1)
        speed_e0, speed_n0 = (whole(1), whole(2))
        flow = east(speed_e0) + north(speed_n0, first_row, last_row)
        fields[0] = whole(0) - depth_step * flow
        fields[1] = speed_e0
        fields[2] = speed_n0

    for i in range(3):
        for r in range(fields.shape[1]):
            start[i, r] = jnp.broadcast_to(fields[i, r : r + 1, :], (SUB, 2 * cols))

    if first:
        each(1, blocks, lambda i: line_copy(i).wait())
        for t in range(ITERS):
            for a in range(n_lat):
                line = lin[a * n_lon + lon][t : t + 1].astype(jnp.int32)
                cells[t * n_lat + a : t * n_lat + a + 1] = line
        slots = cols // blocks
        heard = jnp.concatenate([lin[b] for b in range(blocks)], axis=0)
        kinds = lin.shape[1]
        square = (heard.shape[1], cols)
        from_ids = lax.broadcasted_iota(jnp.int32, square, 0)
        to_ids = lax.broadcasted_iota(jnp.int32, square, 1)
        line_ids = lax.broadcasted_iota(jnp.int32, heard.shape, 0)
        lane_ids = lax.broadcasted_iota(jnp.int32, heard.shape, 1)
        info[...] = jnp.zeros(info.shape, jnp.float32)
        for j in range(share):
            owner = (ens * share + j) * n_lon + lon
            chosen = from_ids == owner * slots + lax.rem(to_ids, slots)
            spread_out = jnp.dot(
                heard,
                chosen.astype(jnp.float32),
                precision=lax.Precision.HIGHEST,
                preferred_element_type=jnp.float32,
            )
            for kind in range(2 * ITERS):
                wanted = line_ids == (lane_ids // slots) * kinds + ITERS + kind
                info[kind : kind + 1, j * cols : (j + 1) * cols] = jnp.sum(
                    jnp.where(wanted, spread_out, 0.0), axis=0, keepdims=True
                )

    def answer_copy(k, i):
        to = lax.rem(here + i, column)
        part_rows = pl.ds(k * SUB, SUB)
        return send(
            outgoing.at[pl.ds((to // n_lat) * share, share), part_rows],
            arrived.at[:, here, part_rows],
            send_y.at[k, i],
            recv_y.at[k, i],
            same_column(to),
        )

    def group(k, carry):
        each(1, n_lat, lambda i: param_copy(k, i).wait())
        for side in range(2):
            each(0, n_lat, lambda i: edge_copy(k, i, side).wait())
        for a in range(n_lat):
            for p in range(2):
                after, before = (goth[k, a, 0, p], goth[k, a, 1, p])
                for r in range(rows):
                    shift = (cols - EDGE * r) % cols
                    right = pltpu.roll(after, shift, 1)
                    left = pltpu.roll(before, (shift + cols - EDGE) % cols, 1)
                    got[k, p, a * rows + r, :, cols : 2 * cols] = jnp.where(
                        lane < EDGE, right, jnp.where(lane >= cols - EDGE, left, 0.0)
                    )
        run_group(k, got, start, height, speed_e, speed_n)
        for a in range(n_lat):
            line = iteration * n_lat + a
            wanted = jnp.broadcast_to(cells[line : line + 1], (SUB, cols))
            lanes = jnp.bitwise_and(wanted, cols - 1)
            where_row = jnp.right_shift(wanted, cols.bit_length() - 1)
            found = jnp.zeros((SUB, cols), jnp.float32)
            for r in range(rows):
                tile = height[a * rows + r + 1, :, 0:cols]
                picked = jnp.take_along_axis(tile, lanes, axis=1)
                found = jnp.where(where_row == r, picked, found)
            outgoing[a, pl.ds(k * SUB, SUB)] = found
        each(1, column, lambda i: answer_copy(k, i).start())
        return carry

    lax.fori_loop(0, groups_here, group, 0)
    for j in range(share):
        arrived[j, pl.ds(here, 1)] = outgoing[pl.ds(ens * share + j, 1)]
    for k in range(groups_here):
        each(1, column, lambda i: answer_copy(k, i).wait())

    members = column * arrived.shape[2]
    predicted = jnp.concatenate(
        [
            jnp.concatenate([arrived[j, s] for s in range(column)], axis=0)
            for j in range(share)
        ],
        axis=1,
    )
    observed = info[iteration : iteration + 1]
    precision = info[ITERS + iteration : ITERS + iteration + 1]
    centre = jnp.sum(predicted, axis=0, keepdims=True) / members
    spread = predicted - centre
    weighted = spread * precision
    extra = lax.broadcasted_iota(jnp.int32, (SUB, share * cols), 0) == 0
    extra = jnp.where(extra, jnp.broadcast_to(observed - centre, extra.shape), 0.0)
    product = lax.dot_general(
        jnp.concatenate([spread, extra], axis=0),
        weighted,
        (((1,), (1,)), ((), ())),
        precision=lax.Precision.HIGHEST,
        preferred_element_type=jnp.float32,
    )
    lines = members // n_ens
    for e in range(n_ens):
        part[e, 0:lines] = product[e * lines : (e + 1) * lines]
        part[e, lines:] = product[members:]

    partner = at(lat, lon, 1 - ens)
    trade = send(part.at[1 - ens], partner_part, send_x.at[0], recv_x.at[0], partner)
    trade.start()
    trade.wait()
    half_sum[...] = part[ens] + partner_part[...]

    def half_copy(i):
        return send(
            half_sum, halves.at[lon], send_z.at[i], recv_z.at[i], at(lat, east_of(i), ens)
        )

    each(1, n_lon, lambda i: half_copy(i).start())
    halves[lon] = half_sum[...]
    each(1, n_lon, lambda i: half_copy(i).wait())
    total = halves[0]
    for b in range(1, n_lon):
        total = total + halves[b]
    part[ens] = total
    finish = send(part.at[ens], gx.at[ens], send_x.at[1], recv_x.at[1], partner)
    finish.start()
    gx[ens] = total
    finish.wait()
    swap.wait()


def ensemble_call(iteration, sizes, own_shape, *operands):
    n_lat, n_lon, n_ens = sizes
    blocks = n_lat * n_lon
    column = n_lat * n_ens
    groups, _, rows, _, cols = own_shape
    groups_here = groups // n_lat
    members = groups * SUB * n_ens
    share = n_lat // n_ens
    all_rows = n_lat * rows
    lines = members // n_ens + SUB
    f32 = jnp.float32
    dma = pltpu.SemaphoreType.DMA
    first = iteration == 0
    outs = [
        jax.ShapeDtypeStruct((n_ens, lines, members), f32),
        jax.ShapeDtypeStruct(own_shape, f32),
    ]
    scratch = []
    if first:
        outs += [
            jax.ShapeDtypeStruct(own_shape, f32),
            jax.ShapeDtypeStruct((3, all_rows, 2 * cols), f32),
            jax.ShapeDtypeStruct((ITERS * n_lat, cols), jnp.int32),
            jax.ShapeDtypeStruct((SUB, share * cols), f32),
        ]
        scratch += [
            VMEM((4, rows, cols), f32),
            VMEM((blocks, rows, cols), f32),
            VMEM((3, n_lat, 3, rows, cols), f32),
            dma((n_lat, 3)),
            dma((n_lat, 3)),
            dma((blocks,)),
            dma((blocks,)),
        ]
    scratch += [
        VMEM((groups_here, 2, all_rows, SUB, 2 * cols), f32),
        VMEM((2, groups, 2, SUB, cols), f32),
        VMEM((groups_here, n_lat, 2, 2, SUB, cols), f32),
        VMEM((3, all_rows, SUB, 2 * cols), f32),
        VMEM((all_rows + 2, SUB, 2 * cols), f32),
        VMEM((all_rows, SUB, 2 * cols), f32),
        VMEM((all_rows + 2, SUB, 2 * cols), f32),
        VMEM((n_lat, groups_here * SUB, cols), f32),
        VMEM((share, column, groups_here * SUB, cols), f32),
        VMEM((n_ens, lines, members), f32),
        VMEM((lines, members), f32),
        VMEM((lines, members), f32),
        VMEM((n_lon, lines, members), f32),
        dma((groups_here, n_lat)),
        dma((groups_here, n_lat)),
        dma((groups_here, n_lat, 2)),
        dma((groups_here, n_lat, 2)),
        dma((1,)),
        dma((1,)),
        dma((groups_here, column)),
        dma((groups_here, column)),
        dma((2,)),
        dma((2,)),
        dma((n_lon,)),
        dma((n_lon,)),
    ]
    return pl.pallas_call(
        functools.partial(ensemble_kernel, iteration, n_lat, n_lon, n_ens),
        out_shape=outs,
        in_specs=[pl.BlockSpec(memory_space=VMEM)] * len(operands),
        out_specs=[pl.BlockSpec(memory_space=VMEM)] * len(outs),
        scratch_shapes=scratch,
        compiler_params=pltpu.CompilerParams(
            collective_id=iteration, has_side_effects=True, vmem_limit_bytes=40 * 2**20
        ),
    )(*operands)


def with_rows(value, rows, start):
    end = start + rows.shape[0]
    pieces = [value[:start]] if start else []
    pieces.append(rows)
    if end < value.shape[0]:
        pieces.append(value[end:])
    return jnp.concatenate(pieces, axis=0)


def inverse_below(matrix):
    size = matrix.shape[1]
    panel = SUB
    row_ids = lax.broadcasted_iota(jnp.int32, (panel, size), 0)
    lane_ids = lax.broadcasted_iota(jnp.int32, (panel, size), 1)
    all_lanes = lax.broadcasted_iota(jnp.int32, matrix.shape, 1)
    for start in range(0, size, panel):
        end = start + panel
        rows = matrix[start:end]
        columns = [
            jnp.broadcast_to(rows[:, start + k : start + k + 1], (panel, size))
            for k in range(panel)
        ]
        inside = jnp.logical_and(lane_ids >= start, lane_ids < end)
        rows = jnp.where(inside, (lane_ids - start == row_ids).astype(jnp.float32), rows)
        for k in range(panel):
            column = columns[k]
            inverse = 1.0 / column[k : k + 1]
            here = row_ids == k

            def reduce(value):
                pivot_row = value[k : k + 1] * inverse
                return jnp.where(here, pivot_row, value - column * pivot_row)

            rows = reduce(rows)
            for later in range(k + 1, panel):
                columns[later] = reduce(columns[later])
        after = jnp.where(
            jnp.logical_and(all_lanes >= start, all_lanes < end), 0.0, matrix
        )
        for k in range(panel):
            after = after - matrix[:, start + k : start + k + 1] * rows[k : k + 1]
        matrix = with_rows(after, rows, start)
    return matrix


def update_kernel(gx, own, other, out):
    ens = lax.axis_index("ens")
    groups, _, rows, _, cols = own.shape
    members = gx.shape[2]
    lines = gx.shape[1] - SUB
    gram = jnp.concatenate([gx[e, 0:lines] for e in range(gx.shape[0])], axis=0)
    ids = [lax.broadcasted_iota(jnp.int32, gram.shape, axis) for axis in (0, 1)]
    unit = (ids[0] == ids[1]).astype(jnp.float32)
    swept = inverse_below(jnp.concatenate([gram / members + unit, gx[0, lines:]], axis=0))
    shift = swept[members : members + 1] / members
    weights = swept[:members] - unit - shift
    centred = weights - jnp.sum(weights, axis=1, keepdims=True) / members
    mine = jnp.where(ens == 0, centred[:lines], centred[lines:])
    mine = jnp.where(ens == 0, mine, pltpu.roll(mine, lines, 1))
    for p in range(2):
        for r in range(rows):
            local = jnp.concatenate([own[g, p, r] for g in range(groups)], axis=0)
            remote = jnp.concatenate([other[g, p, r] for g in range(groups)], axis=0)
            new = local + jnp.dot(
                mine,
                jnp.concatenate([local, remote], axis=0),
                precision=lax.Precision.HIGHEST,
                preferred_element_type=jnp.float32,
            )
            if len(out.shape) == 4:
                out[p, :, r, :] = new
            else:
                for g in range(groups):
                    out[g, p, r] = new[g * SUB : (g + 1) * SUB]


def update_call(shape, *operands):
    return pl.pallas_call(
        update_kernel,
        out_shape=jax.ShapeDtypeStruct(shape, jnp.float32),
        in_specs=[pl.BlockSpec(memory_space=VMEM)] * len(operands),
        out_specs=pl.BlockSpec(memory_space=VMEM),
        compiler_params=pltpu.CompilerParams(vmem_limit_bytes=40 * 2**20),
    )(*operands)


def per_device_columns(sizes, *arguments):
    shape = arguments[0].shape
    own_shape = (shape[1] // SUB, shape[0], shape[2], SUB, shape[3])
    gx, other, own, *known = ensemble_call(0, sizes, own_shape, *arguments)
    for iteration in range(1, ITERS):
        own = update_call(own_shape, gx, own, other)
        gx, other = ensemble_call(iteration, sizes, own_shape, own, *known)
    return update_call(shape, gx, own, other)


def by_members(sizes, parameters, initial_height, initial_speed, obs_slots, *rest):
    n_lat, n_lon, n_ens = sizes
    members_here, rows, cols = parameters.shape[1:]
    fits = (
        n_ens == 2
        and n_lat % n_ens == 0
        and n_lon >= 3
        and members_here % (SUB * n_lat) == 0
        and rows == SUB
        and members_here * n_ens == cols
        and cols == 128
        and EDGE * rows == cols
        and 2 * STEPS <= EDGE
        and ITERS * 3 <= rows
        and obs_slots.shape[2] * obs_slots.shape[3] == cols
    )
    arguments = (parameters, initial_height, initial_speed, obs_slots) + rest
    if fits:
        return per_device_columns(sizes, *arguments)
    return per_device_halo(*arguments)


def solution(mesh):
    placed = (
        P(None, "ens", "lat", "lon"),
        P("lat", "lon"),
        P(None, "lat", "lon"),
        P(None, ("lat", "lon"), None, None),
        P(None, ("lat", "lon"), None, None),
        P(None, ("lat", "lon"), None, None),
    )
    return jax.shard_map(
        functools.partial(by_members, tuple(mesh.shape[a] for a in ("lat", "lon", "ens"))),
        mesh=mesh,
        in_specs=placed,
        out_specs=P(None, "ens", "lat", "lon"),
        check_vma=False,
    )
```

profile of v0, /device:TPU:0, one launch (start us, length us, event | category | flops | bytes accessed | tf_op | source)
XLA Modules:
  0.0 72.0 jit_solution(776496299450937890)
XLA Ops:
  0.0 0.0 copy-start.3
  0.0 0.8 %copy.7.refs_3_ = s32[2,1,16,8]{3,2,1,0:T(8,128)S(1)} copy(s32[2,1,16,8]{2,3,1,0:T(8,128)} %param.9) | data formatting | bytes 2048 | tf_op args[3]
  0.8 0.0 copy-done.3
  0.8 0.0 copy-start.4
  0.8 0.1 copy.8.refs_4_
  0.9 0.6 copy-done.4
  1.5 0.0 copy-start.1
  1.5 0.0 copy-start.2
  1.5 0.1 copy.9.refs_5_
  1.6 0.6 copy-done.1
  2.2 0.0 copy-done.2
  2.2 0.0 copy-start
  2.2 1.0 %copy-done = f32[2,64,8,128]{3,2,1,0:T(8,128)S(1)} copy-done((f32[2,64,8,128]{3,2,1,0:T(8,128)S(1)}, f32[2,64,8,128]{3,2,1,0:T(8,128)}, u32[]{:S(2)}) %copy-start) | copy-done | bytes 524312
  3.2 32.2 %shard_map.64 = (f32[2,72,128]{2,1,0:T(8,128)S(1)}, f32[8,2,8,8,128]{4,3,2,1,0:T(8,128)S(1)}, f32[8,2,8,8,128]{4,3,2,1,0:T(8,128)S(1)}, f32[3,32,256]{2,1,0:T(8,...) custom-call(f32[2,64,8,128]{3,2,1,0:T(8,128)S(1)} %copy-done, f32[8,128]{1,0:T(8,128)S(1)} %copy-done.2, ...), custom_call_target="tpu_custom_call" | custom-call | tf_op jit(solution)/shard_map/pallas_call | solution.py:579
  35.4 5.0 %shard_map.65.refs_0_.own = f32[8,2,8,8,128]{4,3,2,1,0:T(8,128)S(1)} custom-call(f32[2,72,128]{2,1,0:T(8,128)S(1)} %get-tuple-element.13.gx, f32[8,2,8,8,128]{4,3,2,1,0:T(8,128)S(1)} %get-tuple-element.14.own, f32[8,2,8,8,128]{4,3,2,1,0:T(8,128)S(1)} %get-tuple-element.15.other), custom_call_target="tpu_custom_call" | custom-call | tf_op jit(solution)/shard_map/pallas_call | solution.py:668
  40.4 25.8 %shard_map.66 = (f32[2,72,128]{2,1,0:T(8,128)S(1)}, f32[8,2,8,8,128]{4,3,2,1,0:T(8,128)S(1)}) custom-call(f32[8,2,8,8,128]{4,3,2,1,0:T(8,128)S(1)} %shard_map.65.refs_0_.own, f32[3,32,256]{2,1,0:T(8,128)S(1)} %get-tuple-element.16.refs_1_, s32[8,128]{1,0:T(8,128)S(1)} %get-tuple-element.17.refs_2_, f32[8,256]{1,0:T(8,128)S(1)} %get-tuple-element.18.refs_3_), custom_call_target="tpu_custom_call" | custom-call | tf_op jit(solution)/shard_map/pallas_call | solution.py:579
  66.2 5.8 %shard_map.67 = f32[2,64,8,128]{3,2,1,0:T(8,128)} custom-call(f32[2,72,128]{2,1,0:T(8,128)S(1)} %get-tuple-element.19.gx, f32[8,2,8,8,128]{4,3,2,1,0:T(8,128)S(1)} %shard_map.65.refs_0_.own, f32[8,2,8,8,128]{4,3,2,1,0:T(8,128)S(1)} %get-tuple-element.20.other), custom_call_target="tpu_custom_call" | custom-call | tf_op jit(solution)/shard_map/pallas_call | solution.py:668
Async XLA Ops:
  0.0 0.8 %copy-start.3 = (f32[2,1,16,8]{2,3,1,0:T(8,128)S(1)}, f32[2,1,16,8]{2,3,1,0:T(8,128)}, u32[]{:S(2)}) copy-start(f32[2,1,16,8]{2,3,1,0:T(8,128)} %param.10) | copy-start | bytes 3076
  0.8 0.7 copy-start.4
  1.5 0.7 copy-start.1
  1.5 0.7 copy-start.2
  2.2 1.0 %copy-start = (f32[2,64,8,128]{3,2,1,0:T(8,128)S(1)}, f32[2,64,8,128]{3,2,1,0:T(8,128)}, u32[]{:S(2)}) copy-start(f32[2,64,8,128]{3,2,1,0:T(8,128)} %refs_0_.1) | copy-start | bytes 1572868
where the time goes:
time: 72.5 us; the launch traced here: 72 us
  Pallas kernels  68.8 us (95%)
  local copies, waits for them, and re-layouts  3.23 us (4%)
    pallas_call x2, Pallas kernels, ensemble_call(): pl.pallas_call(functools.partial(ensemble_kernel, iteration, n_lat, n_lon...  58 us
    pallas_call x2, Pallas kernels, update_call(): pl.pallas_call(update_kernel, out_shape=jax.ShapeDtypeStruct(shape, jnp.f...  10.8 us
    unnamed x13, local copies, waits for them, and re-layouts  3.23 us

commit v1 on v0

v1 whole, which is shorter than its diff:
```python
import math

import functools

import jax
import jax.numpy as jnp
from jax import lax
from jax.experimental import pallas as pl
from jax.experimental.pallas import tpu as pltpu
from jax.sharding import PartitionSpec as P

STEPS = 6
ITERS = 2


depth_step = 0.7
gravity_step = 0.7
coriolis = 0.1


def padded_2(value, sides, width, wrap):
    for axis, dim in sides:
        peers, length = (lax.axis_size(axis), value.shape[dim])
        up = [(i, (i + 1) % peers) for i in range(peers if wrap else peers - 1)]
        down = [(j, i) for i, j in up]
        last = lax.slice_in_dim(value, length - width, length, axis=dim)
        leading = lax.slice_in_dim(value, 0, width, axis=dim)
        before = lax.ppermute(last, axis, up)
        after = lax.ppermute(leading, axis, down)
        value = jnp.concatenate([before, value, after], axis=dim)
    return value


def wall_rows(padded):
    row_count = padded.shape[-2]
    position = lax.axis_index("lat")
    last_block = lax.axis_size("lat") - 1
    row_ids = lax.broadcasted_iota(jnp.int32, (row_count, 1), 0)
    lower_wall = jnp.logical_and(row_ids == 0, position == 0)
    upper_wall = jnp.logical_and(row_ids == row_count - 1, position == last_block)
    keep_rows = jnp.logical_not(jnp.logical_or(lower_wall, upper_wall))
    return padded * keep_rows.astype(padded.dtype)


def advance(height, speeds, friction, forcing):
    east_padded = padded_2(speeds[0], (("lon", 2),), 1, True)
    north_padded = padded_2(speeds[1], (("lat", 1),), 1, False)
    east_diff = east_padded[:, :, 2:] - east_padded[:, :, :-2]
    north_diff = north_padded[:, 2:, :] - north_padded[:, :-2, :]
    height = height - depth_step * (east_diff + north_diff) + forcing
    padded_height = padded_2(height, (("lat", 1), ("lon", 2)), 1, True)
    padded_height = wall_rows(padded_height)
    slope_east = padded_height[:, 1:-1, 2:] - padded_height[:, 1:-1, :-2]
    slope_north = padded_height[:, 2:, 1:-1] - padded_height[:, :-2, 1:-1]
    eastward = (1.0 - friction) * speeds[0] - gravity_step * slope_east + coriolis * speeds[1]
    northward = (1.0 - friction) * speeds[1] - gravity_step * slope_north - coriolis * speeds[0]
    return (height, jnp.stack([eastward, northward]))


def forward(parameters, initial_height, initial_speed):
    members = parameters.shape[1]
    height = jnp.broadcast_to(initial_height, (members,) + initial_height.shape)
    speeds = jnp.broadcast_to(initial_speed[:, None], (2, members) + initial_height.shape)
    for substep in range(STEPS):
        height, speeds = advance(height, speeds, parameters[0], parameters[1])
    return height


def predict(height, cells):
    flattened = height.reshape(height.shape[0], -1)
    wanted = cells.reshape(-1)
    picked = jnp.take(flattened, jnp.clip(wanted, 0, flattened.shape[1] - 1), axis=1)
    picked = jnp.where(wanted[None, :] >= 0, picked, jnp.float32(0.0))
    return picked.T.reshape(cells.shape[0], -1)


def gram_terms(predicted, observed, precision):
    members = predicted.shape[1]
    centre = jnp.mean(predicted, axis=1, keepdims=True)
    spread = predicted - centre
    weighted = spread * precision[:, None]
    misfit = observed[:, None] - predicted
    gram_part = jnp.dot(spread.T, weighted, precision=lax.Precision.HIGHEST) / members
    cross_part = jnp.dot(weighted.T, misfit, precision=lax.Precision.HIGHEST) / math.sqrt(members)
    return (gram_part, cross_part)


def solve_weights(gram_part, cross_part):
    members = gram_part.shape[0]
    system = jnp.eye(members, dtype=jnp.float32) + gram_part
    factor = jnp.linalg.cholesky(system)
    weights = jax.scipy.linalg.cho_solve((factor, True), cross_part) / math.sqrt(members)
    return weights - jnp.mean(weights, axis=0, keepdims=True)


def per_device_halo(parameters, initial_height, initial_speed, obs_slots, obs_values, obs_precision):
    owners = obs_slots.shape[2]
    slot_count = obs_slots.shape[3]
    members_here = parameters.shape[1]
    member_block = lax.axis_index("ens")
    owner_values, owner_precision = (
        lax.all_to_all(obs_values[:, 0], ("lat", "lon"), split_axis=1, concat_axis=1, tiled=True),
        lax.all_to_all(
            obs_precision[:, 0], ("lat", "lon"), split_axis=1, concat_axis=1, tiled=True
        ),
    )
    for iteration in range(ITERS):
        height = forward(parameters, initial_height, initial_speed)
        outgoing = predict(height, obs_slots[iteration, 0])
        received = outgoing
        observed = owner_values[iteration]
        precision = owner_precision[iteration]
        received = received.reshape(owners, slot_count, members_here)
        gathered = lax.all_gather(received, "ens", axis=2, tiled=True)
        members = gathered.shape[2]
        gram_part, cross_part = gram_terms(
            gathered.reshape(-1, members), observed.reshape(-1), precision.reshape(-1)
        )
        gram_part, cross_part = lax.psum((gram_part, cross_part), ("lat", "lon"))
        centred = solve_weights(gram_part, cross_part)
        local_weights = lax.dynamic_slice_in_dim(
            centred, member_block * members_here, members_here, 1
        )
        starting = jnp.zeros(
            (2, members_here, parameters.shape[2] * parameters.shape[3]), jnp.float32
        )
        pieces = lax.all_gather(parameters, "ens", axis=1, tiled=True)
        stacked = pieces.reshape(pieces.shape[0], pieces.shape[1], -1)
        increment = starting + jnp.einsum(
            "pjc,jm->pmc", stacked, local_weights, precision=lax.Precision.HIGHEST
        )
        parameters = parameters + increment.reshape(parameters.shape)
    return parameters


MESH = pl.DeviceIdType.MESH
VMEM = pltpu.VMEM
EDGE = 16
SUB = 8
CHUNK = 4
VMEM_LIMIT = 40 * 2**20


def east(field):
    width, axis = (field.shape[-1], field.ndim - 1)
    return pltpu.roll(field, width - 1, axis) - pltpu.roll(field, 1, axis)


def north(field, first_row, last_row):
    height = field.shape[0]
    after = jnp.where(last_row, 0.0, pltpu.roll(field, height - 1, 0))
    before = jnp.where(first_row, 0.0, pltpu.roll(field, 1, 0))
    return after - before


def flat_lines(blocks, width):
    count, groups = blocks[0].shape
    lanes = lax.broadcasted_iota(jnp.int32, (groups, width), 1)
    group_ids = lax.broadcasted_iota(jnp.int32, (groups, width), 0)
    spread_out = jnp.dot(
        jnp.concatenate(blocks, axis=0),
        (lanes // count == group_ids).astype(jnp.float32),
        precision=lax.Precision.HIGHEST,
        preferred_element_type=jnp.float32,
    )
    slots = lax.broadcasted_iota(jnp.int32, (count, width), 0)
    lanes = lax.broadcasted_iota(jnp.int32, (count, width), 1)
    keep = lax.rem(lanes, count) == slots
    lines = []
    for n in range(len(blocks)):
        block = spread_out[n * count : (n + 1) * count]
        lines.append(jnp.sum(jnp.where(keep, block, 0.0), axis=0, keepdims=True))
    return lines


def each(start, count, body):
    def step(i, carry):
        body(i)
        return carry

    lax.fori_loop(start, count, step, 0)


def send(src, dst, send_sem, recv_sem, device):
    return pltpu.make_async_remote_copy(
        src_ref=src,
        dst_ref=dst,
        send_sem=send_sem,
        recv_sem=recv_sem,
        device_id=device,
        device_id_type=MESH,
    )


def run_group(k, got, start, height, speed_e, speed_n):
    rows = start.shape[1]
    chunks = [pl.ds(c, CHUNK) for c in range(0, rows, CHUNK)]
    upper = [pl.ds(c + 2, CHUNK) for c in range(0, rows, CHUNK)]
    inner = [pl.ds(c + 1, CHUNK) for c in range(0, rows, CHUNK)]

    def new_speeds(n, keep, old_e, old_n):
        slope_e = east(height[inner[n]])
        slope_n = height[upper[n]] - height[chunks[n]]
        speed_e[chunks[n]] = keep * old_e - gravity_step * slope_e + coriolis * old_n
        speed_n[inner[n]] = keep * old_n - gravity_step * slope_n - coriolis * old_e

    def new_height():
        for n in range(len(chunks)):
            flow = east(speed_e[chunks[n]]) + (speed_n[upper[n]] - speed_n[chunks[n]])
            height[inner[n]] = height[inner[n]] - depth_step * flow + got[k, 1, chunks[n]]

    for n in range(len(chunks)):
        height[inner[n]] = start[0, chunks[n]] + got[k, 1, chunks[n]]
    for n in range(len(chunks)):
        keep = 1.0 - got[k, 0, chunks[n]]
        got[k, 0, chunks[n]] = keep
        new_speeds(n, keep, start[1, chunks[n]], start[2, chunks[n]])

    def middle(step, carry):
        new_height()
        for n in range(len(chunks)):
            new_speeds(n, got[k, 0, chunks[n]], speed_e[chunks[n]], speed_n[inner[n]])
        return carry

    lax.fori_loop(1, STEPS - 1, middle, 0)
    new_height()


def with_rows(value, rows, start):
    end = start + rows.shape[0]
    pieces = [value[:start]] if start else []
    pieces.append(rows)
    if end < value.shape[0]:
        pieces.append(value[end:])
    return jnp.concatenate(pieces, axis=0)


def inverse_below(matrix):
    size = matrix.shape[1]
    panel = SUB
    row_ids = lax.broadcasted_iota(jnp.int32, (panel, size), 0)
    lane_ids = lax.broadcasted_iota(jnp.int32, (panel, size), 1)
    all_lanes = lax.broadcasted_iota(jnp.int32, matrix.shape, 1)
    for start in range(0, size, panel):
        end = start + panel
        rows = matrix[start:end]
        columns = [
            jnp.broadcast_to(rows[:, start + k : start + k + 1], (panel, size))
            for k in range(panel)
        ]
        inside = jnp.logical_and(lane_ids >= start, lane_ids < end)
        rows = jnp.where(inside, (lane_ids - start == row_ids).astype(jnp.float32), rows)
        for k in range(panel):
            column = columns[k]
            inverse = 1.0 / column[k : k + 1]
            here = row_ids == k

            def reduce(value):
                pivot_row = value[k : k + 1] * inverse
                return jnp.where(here, pivot_row, value - column * pivot_row)

            rows = reduce(rows)
            for later in range(k + 1, panel):
                columns[later] = reduce(columns[later])
        after = jnp.where(
            jnp.logical_and(all_lanes >= start, all_lanes < end), 0.0, matrix
        )
        for k in range(panel):
            after = after - matrix[:, start + k : start + k + 1] * rows[k : k + 1]
        matrix = with_rows(after, rows, start)
    return matrix


def member_weights(gx, ens):
    members = gx.shape[2]
    lines = gx.shape[1] - SUB
    gram = jnp.concatenate([gx[e, 0:lines] for e in range(gx.shape[0])], axis=0)
    ids = [lax.broadcasted_iota(jnp.int32, gram.shape, axis) for axis in (0, 1)]
    unit = (ids[0] == ids[1]).astype(jnp.float32)
    swept = inverse_below(jnp.concatenate([gram / members + unit, gx[0, lines:]], axis=0))
    shift = swept[members : members + 1] / members
    weights = swept[:members] - unit - shift
    centred = weights - jnp.sum(weights, axis=1, keepdims=True) / members
    mine = jnp.where(ens == 0, centred[:lines], centred[lines:])
    return jnp.where(ens == 0, mine, pltpu.roll(mine, lines, 1))


def updated_rows(mine, own, other, store):
    groups, _, rows, _, cols = own.shape
    for p in range(2):
        for r in range(0, rows, 2):
            pair, local = ([], [])
            for q in (r, r + 1):
                local.append(jnp.concatenate([own[g, p, q] for g in range(groups)], axis=0))
                remote = [other[g, p, q] for g in range(groups)]
                pair.append(jnp.concatenate([local[-1]] + remote, axis=0))
            added = jnp.dot(
                mine,
                jnp.concatenate(pair, axis=1),
                precision=lax.Precision.HIGHEST,
                preferred_element_type=jnp.float32,
            )
            for q in range(2):
                store(p, r + q, local[q] + added[:, q * cols : (q + 1) * cols])


def ensemble_kernel(n_lat, n_lon, n_ens, *refs):
    params, start_height, start_speed, slots_in, values_in, precision_in = refs[:6]
    gx_out, own_out, other_out = refs[6:9]
    owns, others, gxs, aux, lin, fin, slots_here, values_here, precision_here = refs[9:18]
    cells, info, start, height, speed_e, speed_n = refs[18:24]
    gots, edges, goths, outgoing, arriveds, part, partner_parts, half_sum, halves_all = refs[24:33]
    load, send_a, recv_a, send_l, recv_l, send_p, recv_p, send_h, recv_h = refs[33:42]
    send_o, recv_o, send_y, recv_y, send_x, recv_x, send_z, recv_z = refs[42:]
    lat, lon, ens = (lax.axis_index("lat"), lax.axis_index("lon"), lax.axis_index("ens"))
    blocks = n_lat * n_lon
    me = lat * n_lon + lon
    column = n_lat * n_ens
    here = ens * n_lat + lat
    groups, _, rows, _, cols = own_out.shape
    all_rows = n_lat * rows
    groups_here = groups // n_lat
    share = n_lat // n_ens
    lane = lax.broadcasted_iota(jnp.int32, (SUB, cols), 1)
    own_rows = pl.ds(lat * rows, rows)

    def at(lat_to, lon_to, ens_to):
        return {"lat": lat_to, "lon": lon_to, "ens": ens_to}

    def same_column(flat):
        return at(lax.rem(flat, n_lat), lon, flat // n_lat)

    def same_core(block):
        return at(block // n_lon, lax.rem(block, n_lon), ens)

    def east_of(d):
        return lax.rem(lon + d + n_lon, n_lon)

    partner = at(lat, lon, 1 - ens)
    barrier = pltpu.get_barrier_semaphore()

    def greet(device):
        pl.semaphore_signal(barrier, inc=1, device_id=device, device_id_type=MESH)

    each(1, blocks, lambda i: greet(same_core(lax.rem(me + i, blocks))))
    each(0, n_lat, lambda i: greet(at(i, lon, 1 - ens)))

    small = [
        pltpu.make_async_copy(src, dst, load.at[n])
        for n, (src, dst) in enumerate(
            (
                (slots_in, slots_here),
                (values_in, values_here),
                (precision_in, precision_here),
                (start_height, aux.at[0]),
                (start_speed, aux.at[1:3]),
            )
        )
    ]
    large = [
        pltpu.make_async_copy(
            params.at[p, :, :, r, :], owns.at[0, :, p, r], load.at[len(small) + p * rows + r]
        )
        for p in range(2)
        for r in range(rows)
    ]
    for copy in small + large:
        copy.start()
    zero_row = jnp.zeros((1, SUB, 2 * cols), jnp.float32)
    for ref in (height, speed_n):
        ref[0:1] = zero_row
        ref[all_rows + 1 : all_rows + 2] = zero_row
    info[...] = jnp.zeros(info.shape, jnp.float32)
    for copy in small:
        copy.wait()
    lines = flat_lines(
        [
            ref[t, 0].astype(jnp.float32)
            for ref in (slots_here, values_here, precision_here)
            for t in range(ITERS)
        ],
        cols,
    )
    lines.append(jnp.zeros((rows - len(lines), cols), jnp.float32))
    aux[3] = jnp.concatenate(lines, axis=0)
    for copy in large:
        copy.wait()

    def field_copy(i, d):
        return send(
            aux.at[0:3],
            fin.at[d % 3, lat],
            send_a.at[i, d % 3],
            recv_a.at[i, d % 3],
            at(lax.rem(lat + i, n_lat), east_of(-d), ens),
        )

    def line_copy(i):
        return send(
            aux.at[3],
            lin.at[me],
            send_l.at[i],
            recv_l.at[i],
            same_core(lax.rem(me + i, blocks)),
        )

    def run_iteration(t, own, other, gx):
        got, goth, arrived = (gots.at[t], goths.at[t], arriveds.at[t])
        partner_part, halves = (partner_parts.at[t], halves_all.at[t])

        def param_copy(k, i):
            to = lax.rem(lat + i, n_lat)
            return send(
                own.at[to * groups_here + k],
                got.at[k, :, own_rows, :, pl.ds(0, cols)],
                send_p.at[t, k, i],
                recv_p.at[t, k, i],
                at(to, lon, ens),
            )

        def edge_copy(k, i, side):
            to = lax.rem(lat + i, n_lat)
            return send(
                edges.at[side, to * groups_here + k],
                goth.at[k, lat, side],
                send_h.at[t, k, i, side],
                recv_h.at[t, k, i, side],
                at(to, east_of(2 * side - 1), ens),
            )

        swap = send(own, other, send_o.at[t], recv_o.at[t], partner)

        def pack_edges(g):
            for p in range(2):
                left = jnp.zeros((SUB, cols), jnp.float32)
                right = left
                for r in range(rows):
                    tile = own[g, p, r]
                    here_lanes = lane // EDGE == r
                    left = jnp.where(here_lanes, pltpu.roll(tile, EDGE * r, 1), left)
                    shift = (EDGE * r + EDGE) % cols
                    right = jnp.where(here_lanes, pltpu.roll(tile, shift, 1), right)
                edges[0, g, p] = left
                edges[1, g, p] = right

        if t == 0:
            for g in range(groups):
                pack_edges(g)
            pl.semaphore_wait(barrier, blocks - 1 + n_lat)
            each(1, n_lat, lambda i: field_copy(i, 0).start())
            for d in (1, -1):
                each(0, n_lat, lambda i: field_copy(i, d).start())
        for k in range(groups_here):
            each(1, n_lat, lambda i: param_copy(k, i).start())
            if t and k == 0:
                for g in range(groups):
                    pack_edges(g)
            for side in range(2):
                each(0, n_lat, lambda i: edge_copy(k, i, side).start())
            if t == 0 and k == 0:
                each(1, blocks, lambda i: line_copy(i).start())
        swap.start()
        for k in range(groups_here):
            got[k, :, own_rows, :, 0:cols] = own[lat * groups_here + k]

        if t == 0:
            for i in range(3):
                fin[0, pl.ds(lat, 1), i] = aux[i : i + 1]
            lin[pl.ds(me, 1)] = aux[3:4]
            each(1, n_lat, lambda i: field_copy(i, 0).wait())
            for d in (1, -1):
                each(0, n_lat, lambda i: field_copy(i, d).wait())

            def whole(i):
                lines = []
                for a in range(n_lat):
                    after, before = (fin[1, a, i], fin[2, a, i])
                    outer = jnp.where(
                        lane < EDGE, after, jnp.where(lane >= cols - EDGE, before, 0.0)
                    )
                    lines.append(jnp.concatenate([fin[0, a, i], outer], axis=1))
                return jnp.concatenate(lines, axis=0)

            row_ids = lax.broadcasted_iota(jnp.int32, (all_rows, 2 * cols), 0)
            first_row, last_row = (row_ids == 0, row_ids == all_rows - 1)
            speed_e0, speed_n0 = (whole(1), whole(2))
            flow = east(speed_e0) + north(speed_n0, first_row, last_row)
            for i, field in enumerate((whole(0) - depth_step * flow, speed_e0, speed_n0)):
                for r in range(all_rows):
                    start[i, r] = jnp.broadcast_to(field[r : r + 1], (SUB, 2 * cols))
            each(1, blocks, lambda i: line_copy(i).wait())
            for n in range(ITERS):
                for a in range(n_lat):
                    line = lin[a * n_lon + lon][n : n + 1].astype(jnp.int32)
                    cells[n * n_lat + a : n * n_lat + a + 1] = line

        def answer_copy(k, i):
            to = lax.rem(here + i, column)
            part_rows = pl.ds(k * SUB, SUB)
            return send(
                outgoing.at[pl.ds((to // n_lat) * share, share), part_rows],
                arrived.at[:, here, part_rows],
                send_y.at[t, k, i],
                recv_y.at[t, k, i],
                same_column(to),
            )

        def group(k, carry):
            each(1, n_lat, lambda i: param_copy(k, i).wait())
            for side in range(2):
                each(0, n_lat, lambda i: edge_copy(k, i, side).wait())
            for a in range(n_lat):
                for p in range(2):
                    after, before = (goth[k, a, 0, p], goth[k, a, 1, p])
                    for r in range(rows):
                        shift = (cols - EDGE * r) % cols
                        right = pltpu.roll(after, shift, 1)
                        left = pltpu.roll(before, (shift + cols - EDGE) % cols, 1)
                        got[k, p, a * rows + r, :, cols : 2 * cols] = jnp.where(
                            lane < EDGE, right, jnp.where(lane >= cols - EDGE, left, 0.0)
                        )
            run_group(k, got, start, height, speed_e, speed_n)
            for a in range(n_lat):
                line = t * n_lat + a
                wanted = jnp.broadcast_to(cells[line : line + 1], (SUB, cols))
                lanes = jnp.bitwise_and(wanted, cols - 1)
                where_row = jnp.right_shift(wanted, cols.bit_length() - 1)
                found = jnp.zeros((SUB, cols), jnp.float32)
                for r in range(rows):
                    tile = height[a * rows + r + 1, :, 0:cols]
                    picked = jnp.take_along_axis(tile, lanes, axis=1)
                    found = jnp.where(where_row == r, picked, found)
                outgoing[a, pl.ds(k * SUB, SUB)] = found
            each(1, column, lambda i: answer_copy(k, i).start())
            return carry

        lax.fori_loop(0, groups_here, group, 0)
        for j in range(share):
            arrived[j, pl.ds(here, 1)] = outgoing[pl.ds(ens * share + j, 1)]
        if t == 0:
            slots = cols // blocks
            heard = jnp.concatenate([lin[b] for b in range(blocks)], axis=0)
            kinds = lin.shape[1]
            square = (heard.shape[1], cols)
            from_ids = lax.broadcasted_iota(jnp.int32, square, 0)
            to_ids = lax.broadcasted_iota(jnp.int32, square, 1)
            line_ids = lax.broadcasted_iota(jnp.int32, heard.shape, 0)
            lane_ids = lax.broadcasted_iota(jnp.int32, heard.shape, 1)
            for j in range(share):
                owner = (ens * share + j) * n_lon + lon
                chosen = from_ids == owner * slots + lax.rem(to_ids, slots)
                spread_out = jnp.dot(
                    heard,
                    chosen.astype(jnp.float32),
                    precision=lax.Precision.HIGHEST,
                    preferred_element_type=jnp.float32,
                )
                for kind in range(2 * ITERS):
                    wanted = line_ids == (lane_ids // slots) * kinds + ITERS + kind
                    info[kind : kind + 1, j * cols : (j + 1) * cols] = jnp.sum(
                        jnp.where(wanted, spread_out, 0.0), axis=0, keepdims=True
                    )
        for k in range(groups_here):
            each(1, column, lambda i: answer_copy(k, i).wait())

        members = column * arrived.shape[2]
        predicted = jnp.concatenate(
            [
                jnp.concatenate([arrived[j, s] for s in range(column)], axis=0)
                for j in range(share)
            ],
            axis=1,
        )
        observed = info[t : t + 1]
        precision = info[ITERS + t : ITERS + t + 1]
        centre = jnp.sum(predicted, axis=0, keepdims=True) / members
        spread = predicted - centre
        weighted = spread * precision
        extra = lax.broadcasted_iota(jnp.int32, (SUB, share * cols), 0) == 0
        extra = jnp.where(extra, jnp.broadcast_to(observed - centre, extra.shape), 0.0)
        product = lax.dot_general(
            jnp.concatenate([spread, extra], axis=0),
            weighted,
            (((1,), (1,)), ((), ())),
            precision=lax.Precision.HIGHEST,
            preferred_element_type=jnp.float32,
        )
        lines = members // n_ens
        for e in range(n_ens):
            part[e, 0:lines] = product[e * lines : (e + 1) * lines]
            part[e, lines:] = product[members:]

        trade = send(part.at[1 - ens], partner_part, send_x.at[t, 0], recv_x.at[t, 0], partner)
        trade.start()
        trade.wait()
        half_sum[...] = part[ens] + partner_part[...]

        def half_copy(i):
            return send(
                half_sum,
                halves.at[lon],
                send_z.at[t, i],
                recv_z.at[t, i],
                at(lat, east_of(i), ens),
            )

        each(1, n_lon, lambda i: half_copy(i).start())
        halves[lon] = half_sum[...]
        each(1, n_lon, lambda i: half_copy(i).wait())
        total = halves[0]
        for b in range(1, n_lon):
            total = total + halves[b]
        half_sum[...] = total
        finish = send(half_sum, gx.at[ens], send_x.at[t, 1], recv_x.at[t, 1], partner)
        finish.start()
        gx[ens] = total
        swap.wait()
        finish.wait()

    for t in range(ITERS):
        last = t == ITERS - 1
        own = own_out if last and t else owns.at[t]
        other, gx = (other_out, gx_out) if last else (others.at[t], gxs.at[t])
        run_iteration(t, own, other, gx)
        if not last:
            new = own_out if t + 1 == ITERS - 1 else owns.at[t + 1]

            def store(p, r, value, new=new):
                for g in range(groups):
                    new[g, p, r] = value[g * SUB : (g + 1) * SUB]

            updated_rows(member_weights(gx, ens), own, other, store)


def ensemble_call(sizes, own_shape, *operands):
    n_lat, n_lon, n_ens = sizes
    blocks = n_lat * n_lon
    column = n_lat * n_ens
    groups, _, rows, _, cols = own_shape
    groups_here = groups // n_lat
    members = groups * SUB * n_ens
    share = n_lat // n_ens
    all_rows = n_lat * rows
    lines = members // n_ens + SUB
    f32 = jnp.float32
    dma = pltpu.SemaphoreType.DMA
    gx_shape = (n_ens, lines, members)
    outs = [jax.ShapeDtypeStruct(shape, f32) for shape in (gx_shape, own_shape, own_shape)]

    def both(shape):
        return [dma(shape), dma(shape)]

    scratch = [
        VMEM((max(ITERS - 1, 1),) + own_shape, f32),
        VMEM((max(ITERS - 1, 1),) + own_shape, f32),
        VMEM((max(ITERS - 1, 1),) + gx_shape, f32),
        VMEM((4, rows, cols), f32),
        VMEM((blocks, rows, cols), f32),
        VMEM((3, n_lat, 3, rows, cols), f32),
    ]
    scratch += [VMEM(obs.shape, obs.dtype) for obs in operands[3:]]
    scratch += [
        VMEM((ITERS * n_lat, cols), jnp.int32),
        VMEM((SUB, share * cols), f32),
        VMEM((3, all_rows, SUB, 2 * cols), f32),
        VMEM((all_rows + 2, SUB, 2 * cols), f32),
        VMEM((all_rows, SUB, 2 * cols), f32),
        VMEM((all_rows + 2, SUB, 2 * cols), f32),
        VMEM((ITERS, groups_here, 2, all_rows, SUB, 2 * cols), f32),
        VMEM((2, groups, 2, SUB, cols), f32),
        VMEM((ITERS, groups_here, n_lat, 2, 2, SUB, cols), f32),
        VMEM((n_lat, groups_here * SUB, cols), f32),
        VMEM((ITERS, share, column, groups_here * SUB, cols), f32),
        VMEM(gx_shape, f32),
        VMEM((ITERS, lines, members), f32),
        VMEM((lines, members), f32),
        VMEM((ITERS, n_lon, lines, members), f32),
        dma((5 + 2 * rows,)),
    ]
    for shape in (
        (n_lat, 3),
        (blocks,),
        (ITERS, groups_here, n_lat),
        (ITERS, groups_here, n_lat, 2),
        (ITERS,),
        (ITERS, groups_here, column),
        (ITERS, 2),
        (ITERS, n_lon),
    ):
        scratch += both(shape)
    return pl.pallas_call(
        functools.partial(ensemble_kernel, n_lat, n_lon, n_ens),
        out_shape=outs,
        in_specs=[pl.BlockSpec(memory_space=pltpu.HBM)] * len(operands),
        out_specs=[pl.BlockSpec(memory_space=VMEM)] * len(outs),
        scratch_shapes=scratch,
        compiler_params=pltpu.CompilerParams(
            collective_id=0, has_side_effects=True, vmem_limit_bytes=VMEM_LIMIT
        ),
    )(*operands)


def update_kernel(gx, own, other, out):
    def store(p, r, value):
        out[p, :, r, :] = value

    updated_rows(member_weights(gx, lax.axis_index("ens")), own, other, store)


def update_call(shape, *operands):
    return pl.pallas_call(
        update_kernel,
        out_shape=jax.ShapeDtypeStruct(shape, jnp.float32),
        in_specs=[pl.BlockSpec(memory_space=VMEM)] * len(operands),
        out_specs=pl.BlockSpec(memory_space=VMEM),
        compiler_params=pltpu.CompilerParams(vmem_limit_bytes=40 * 2**20),
    )(*operands)


def per_device_columns(sizes, parameters, initial_height, initial_speed, *observations):
    shape = parameters.shape
    own_shape = (shape[1] // SUB, shape[0], shape[2], SUB, shape[3])
    grouped = parameters.reshape(shape[0], shape[1] // SUB, SUB, shape[2], shape[3])
    turned = [jnp.transpose(obs, (0, 1, 3, 2)) for obs in observations]
    operands = [grouped, initial_height, initial_speed] + turned
    operands = [pltpu.with_memory_space_constraint(x, pltpu.HBM) for x in operands]
    gathered = ensemble_call(sizes, own_shape, *operands)
    return update_call(shape, *gathered)


def by_members(sizes, parameters, initial_height, initial_speed, obs_slots, *rest):
    n_lat, n_lon, n_ens = sizes
    members_here, rows, cols = parameters.shape[1:]
    fits = (
        n_ens == 2
        and n_lat % n_ens == 0
        and n_lon >= 3
        and members_here % (SUB * n_lat) == 0
        and rows == SUB
        and members_here * n_ens == cols
        and cols == 128
        and EDGE * rows == cols
        and 2 * STEPS <= EDGE
        and ITERS * 3 <= rows
        and obs_slots.shape[2] * obs_slots.shape[3] == cols
        and obs_slots.shape[3] == SUB
        and ITERS > 1
    )
    arguments = (parameters, initial_height, initial_speed, obs_slots) + rest
    if fits:
        return per_device_columns(sizes, *arguments)
    return per_device_halo(*arguments)


def solution(mesh):
    placed = (
        P(None, "ens", "lat", "lon"),
        P("lat", "lon"),
        P(None, "lat", "lon"),
        P(None, ("lat", "lon"), None, None),
        P(None, ("lat", "lon"), None, None),
        P(None, ("lat", "lon"), None, None),
    )
    return jax.shard_map(
        functools.partial(by_members, tuple(mesh.shape[a] for a in ("lat", "lon", "ens"))),
        mesh=mesh,
        in_specs=placed,
        out_specs=P(None, "ens", "lat", "lon"),
        check_vma=False,
    )
```

time: 72.5 us -> 66 us (0.910)
  local copies, waits for them, and re-layouts: 3.23 us -> 0 us
  Pallas kernels: 68.8 us -> 65.8 us
    pallas_call x2 -> x1, Pallas kernels: 10.8 us -> 5.52 us  [update_call(): pl.pallas_call(update_kernel, out_shape=jax.ShapeDtypeStruct(shape, jnp.f...]
    unnamed x13 -> x0, local copies, waits for them, and re-layouts: 3.23 us -> none
    pallas_call x2 -> x1, Pallas kernels: 58 us -> 60.2 us  [ensemble_call(): pl.pallas_call(functools.partial(ensemble_kernel, n_lat, n_lon, n_ens), o...]
where the time goes in v1:
time: 66 us; the launch traced here: 65.8 us
  Pallas kernels  65.8 us (100%)
    pallas_call x1, Pallas kernels, ensemble_call(): pl.pallas_call(functools.partial(ensemble_kernel, n_lat, n_lon, n_ens), o...  60.2 us
    pallas_call x1, Pallas kernels, update_call(): pl.pallas_call(update_kernel, out_shape=jax.ShapeDtypeStruct(shape, jnp.f...  5.52 us

profile of v1, /device:TPU:0, one launch (start us, length us, event | category | flops | bytes accessed | tf_op | source)
XLA Modules:
  0.0 65.8 jit_solution(8346622761704849995)
XLA Ops:
  0.0 60.2 %shard_map.64 = (f32[2,72,128]{2,1,0:T(8,128)S(1)}, f32[8,2,8,8,128]{4,3,2,1,0:T(8,128)S(1)}, f32[8,2,8,8,128]{4,3,2,1,0:T(8,128)S(1)}) custom-call(f32[2,8,8,8,128]{4,3,2,1,0:T(8,128)} %bitcast.4, f32[8,128]{1,0:T(8,128)} %refs_1_.1, f32[2,8,128]{2,1,0:T(8,128)} %refs_2_.1, s32[2,1,8,16]{3,2,1,0:T(8,128)} %bitcast.5, f32[2,1,8,16]{3,2,1,0:T(8,128)} %bitcast.6, ...), custom_call_target="tpu_custom_call" | custom-call | tf_op jit(solution)/shard_map/pallas_call | solution.py:691
  60.2 5.5 %shard_map.65 = f32[2,64,8,128]{3,2,1,0:T(8,128)} custom-call(f32[2,72,128]{2,1,0:T(8,128)S(1)} %get-tuple-element.8.gx, f32[8,2,8,8,128]{4,3,2,1,0:T(8,128)S(1)} %get-tuple-element.9.own, f32[8,2,8,8,128]{4,3,2,1,0:T(8,128)S(1)} %get-tuple-element.10.other), custom_call_target="tpu_custom_call" | custom-call | tf_op jit(solution)/shard_map/pallas_call | solution.py:711

commit v2 on v1

--- a/solution.py
+++ b/solution.py
@@ -226,63 +226,125 @@
     new_height()
 
 
-def with_rows(value, rows, start):
-    end = start + rows.shape[0]
-    pieces = [value[:start]] if start else []
-    pieces.append(rows)
-    if end < value.shape[0]:
-        pieces.append(value[end:])
-    return jnp.concatenate(pieces, axis=0)
-
-
 def inverse_below(matrix):
     size = matrix.shape[1]
-    panel = SUB
-    row_ids = lax.broadcasted_iota(jnp.int32, (panel, size), 0)
-    lane_ids = lax.broadcasted_iota(jnp.int32, (panel, size), 1)
-    all_lanes = lax.broadcasted_iota(jnp.int32, matrix.shape, 1)
-    for start in range(0, size, panel):
-        end = start + panel
-        rows = matrix[start:end]
-        columns = [
-            jnp.broadcast_to(rows[:, start + k : start + k + 1], (panel, size))
-            for k in range(panel)
+    strip = size // 2 // SUB
+    row_ids = lax.broadcasted_iota(jnp.int32, (SUB, size), 0)
+    lane_ids = lax.broadcasted_iota(jnp.int32, (SUB, size), 1)
+    zero = jnp.zeros((SUB, size), jnp.float32)
+    tiles = [matrix[n * SUB : (n + 1) * SUB] for n in range(matrix.shape[0] // SUB)]
+
+    def columns_of(tile, start):
+        return [
+            jnp.broadcast_to(tile[:, start + k : start + k + 1], (SUB, size))
+            for k in range(SUB)
         ]
-        inside = jnp.logical_and(lane_ids >= start, lane_ids < end)
-        rows = jnp.where(inside, (lane_ids - start == row_ids).astype(jnp.float32), rows)
-        for k in range(panel):
-            column = columns[k]
-            inverse = 1.0 / column[k : k + 1]
-            here = row_ids == k
-
-            def reduce(value):
-                pivot_row = value[k : k + 1] * inverse
-                return jnp.where(here, pivot_row, value - column * pivot_row)
-
-            rows = reduce(rows)
-            for later in range(k + 1, panel):
-                columns[later] = reduce(columns[later])
-        after = jnp.where(
-            jnp.logical_and(all_lanes >= start, all_lanes < end), 0.0, matrix
-        )
-        for k in range(panel):
-            after = after - matrix[:, start + k : start + k + 1] * rows[k : k + 1]
-        matrix = with_rows(after, rows, start)
-    return matrix
+
+    def less_rows(tile, band, columns, rows):
+        tile = jnp.where(band, 0.0, tile)
+        for k in range(SUB):
+            tile = tile - columns[k] * rows[k : k + 1]
+        return tile
+
+    for base in range(0, size // SUB, strip):
+        inner = tiles[base : base + strip]
+        columns = columns_of(inner[0], base * SUB)
+        for n in range(strip):
+            start = (base + n) * SUB
+            band = jnp.logical_and(lane_ids >= start, lane_ids < start + SUB)
+            unit = (lane_ids - start == row_ids).astype(jnp.float32)
+            rows = jnp.where(band, unit, inner[n])
+            follows = n + 1 < strip
+            ahead = []
+            if follows:
+                ahead = columns_of(inner[n], start + SUB)
+                below = columns_of(inner[n + 1], start)
+                later = columns_of(inner[n + 1], start + SUB)
+            for k in range(SUB):
+                column = columns[k]
+                inverse = 1.0 / column[k : k + 1]
+                here = row_ids == k
+
+                def reduce(value):
+                    pivot_row = value[k : k + 1] * inverse
+                    return jnp.where(here, pivot_row, value - column * pivot_row)
+
+                for other in range(k + 1, SUB):
+                    columns[other] = reduce(columns[other])
+                ahead = [reduce(value) for value in ahead]
+                rows = reduce(rows)
+            after = list(inner)
+            after[n] = rows
+            if follows:
+                after[n + 1] = less_rows(inner[n + 1], band, below, rows)
+                for k in range(SUB):
+                    later = [
+                        value - below[k] * line[k : k + 1] for value, line in zip(later, ahead)
+                    ]
+                columns = later
+            for m in range(strip):
+                if m != n and not (follows and m == n + 1):
+                    after[m] = less_rows(inner[m], band, columns_of(inner[m], start), rows)
+            inner = after
+        outer = [m for m in range(len(tiles)) if not base <= m < base + strip]
+        lines = [
+            inner[m - base] if base <= m < base + strip else zero for m in range(size // SUB)
+        ]
+        product = jnp.dot(
+            jnp.concatenate([tiles[m] for m in outer], axis=0),
+            jnp.concatenate(lines, axis=0),
+            precision=lax.Precision.HIGHEST,
+            preferred_element_type=jnp.float32,
+        )
+        band = jnp.logical_and(lane_ids >= base * SUB, lane_ids < (base + strip) * SUB)
+        for n, m in enumerate(outer):
+            tiles[m] = jnp.where(band, 0.0, tiles[m]) - product[n * SUB : (n + 1) * SUB]
+        tiles[base : base + strip] = inner
+    return jnp.concatenate(tiles, axis=0)
+
+
+def packed_halves(product, n_ens):
+    half = product.shape[1] // 2
+    row_ids = lax.broadcasted_iota(jnp.int32, (half, 2 * half), 0)
+    lane_ids = lax.broadcasted_iota(jnp.int32, (half, 2 * half), 1)
+    top, bottom = (product[0:half], product[half : 2 * half])
+    dense = jnp.where(lane_ids <= row_ids + half, bottom, pltpu.roll(top, half, 1))
+    diagonal = jnp.sum(jnp.where(lane_ids == row_ids, top, 0.0), axis=0, keepdims=True)
+    tail = jnp.where(row_ids[0:SUB] == 1, diagonal, product[2 * half :])
+    lines = half // n_ens
+    return [
+        jnp.concatenate([dense[e * lines : (e + 1) * lines], tail], axis=0)
+        for e in range(n_ens)
+    ]
+
+
+def unpacked(parts):
+    half = sum(part.shape[0] - SUB for part in parts)
+    dense = jnp.concatenate([part[: part.shape[0] - SUB] for part in parts], axis=0)
+    tail = parts[0][parts[0].shape[0] - SUB :]
+    row_ids = lax.broadcasted_iota(jnp.int32, (half, 2 * half), 0)
+    lane_ids = lax.broadcasted_iota(jnp.int32, (half, 2 * half), 1)
+    turned = jnp.concatenate([dense, dense], axis=0).T
+    upper = jnp.where(lane_ids > row_ids, pltpu.roll(dense, half, 1), turned[half:])
+    upper = jnp.where(lane_ids == row_ids, tail[1:2], upper)
+    top = jnp.where(lane_ids >= half, turned[:half], upper)
+    bottom = jnp.where(lane_ids <= row_ids + half, dense, turned[half:])
+    return jnp.concatenate([top, bottom], axis=0), tail[0:1]
 
 
 def member_weights(gx, ens):
     members = gx.shape[2]
-    lines = gx.shape[1] - SUB
-    gram = jnp.concatenate([gx[e, 0:lines] for e in range(gx.shape[0])], axis=0)
+    half = members // 2
+    gram, line = unpacked([gx[e] for e in range(gx.shape[0])])
     ids = [lax.broadcasted_iota(jnp.int32, gram.shape, axis) for axis in (0, 1)]
     unit = (ids[0] == ids[1]).astype(jnp.float32)
-    swept = inverse_below(jnp.concatenate([gram / members + unit, gx[0, lines:]], axis=0))
+    line = jnp.broadcast_to(line, (SUB, members))
+    swept = inverse_below(jnp.concatenate([gram / members + unit, line], axis=0))
     shift = swept[members : members + 1] / members
     weights = swept[:members] - unit - shift
     centred = weights - jnp.sum(weights, axis=1, keepdims=True) / members
-    mine = jnp.where(ens == 0, centred[:lines], centred[lines:])
-    return jnp.where(ens == 0, mine, pltpu.roll(mine, lines, 1))
+    mine = jnp.where(ens == 0, centred[:half], centred[half:])
+    return jnp.where(ens == 0, mine, pltpu.roll(mine, half, 1))
 
 
 def updated_rows(mine, own, other, store):
@@ -585,10 +647,8 @@
             precision=lax.Precision.HIGHEST,
             preferred_element_type=jnp.float32,
         )
-        lines = members // n_ens
-        for e in range(n_ens):
-            part[e, 0:lines] = product[e * lines : (e + 1) * lines]
-            part[e, lines:] = product[members:]
+        for e, piece in enumerate(packed_halves(product, n_ens)):
+            part[e] = piece
 
         trade = send(part.at[1 - ens], partner_part, send_x.at[t, 0], recv_x.at[t, 0], partner)
         trade.start()
@@ -641,7 +701,7 @@
     members = groups * SUB * n_ens
     share = n_lat // n_ens
     all_rows = n_lat * rows
-    lines = members // n_ens + SUB
+    lines = members // 2 // n_ens + SUB
     f32 = jnp.float32
     dma = pltpu.SemaphoreType.DMA
     gx_shape = (n_ens, lines, members)
@@ -700,11 +760,18 @@
     )(*operands)
 
 
-def update_kernel(gx, own, other, out):
+def update_kernel(gx, own, other, out, new, sems):
+    copies = [pltpu.make_async_copy(new.at[p], out.at[p], sems.at[p]) for p in range(2)]
+    rows = own.shape[2]
+
     def store(p, r, value):
-        out[p, :, r, :] = value
+        new[p, :, r, :] = value
+        if r == rows - 1:
+            copies[p].start()
 
     updated_rows(member_weights(gx, lax.axis_index("ens")), own, other, store)
+    for copy in copies:
+        copy.wait()
 
 
 def update_call(shape, *operands):
@@ -712,8 +779,9 @@
         update_kernel,
         out_shape=jax.ShapeDtypeStruct(shape, jnp.float32),
         in_specs=[pl.BlockSpec(memory_space=VMEM)] * len(operands),
-        out_specs=pl.BlockSpec(memory_space=VMEM),
-        compiler_params=pltpu.CompilerParams(vmem_limit_bytes=40 * 2**20),
+        out_specs=pl.BlockSpec(memory_space=pltpu.HBM),
+        scratch_shapes=[VMEM(shape, jnp.float32), pltpu.SemaphoreType.DMA((2,))],
+        compiler_params=pltpu.CompilerParams(vmem_limit_bytes=VMEM_LIMIT),
     )(*operands)
 
 

time: 66 us -> 63.2 us (0.958)
  Pallas kernels: 65.8 us -> 63 us
    pallas_call x1, Pallas kernels: 60.2 us -> 58.1 us  [ensemble_call(): pl.pallas_call(functools.partial(ensemble_kernel, n_lat, n_lon, n_ens), o...]
where the time goes in v2:
time: 63.2 us; the launch traced here: 63 us
  Pallas kernels  63 us (100%)
    pallas_call x1, Pallas kernels, ensemble_call(): pl.pallas_call(functools.partial(ensemble_kernel, n_lat, n_lon, n_ens), o...  58.1 us
    pallas_call x1, Pallas kernels, update_call(): pl.pallas_call(update_kernel, out_shape=jax.ShapeDtypeStruct(shape, jnp.f...  4.87 us

profile of v2, /device:TPU:0, one launch (start us, length us, event | category | flops | bytes accessed | tf_op | source)
XLA Modules:
  0.0 63.0 jit_solution(9516927178588270268)
XLA Ops:
  0.0 58.1 %shard_map.64 = (f32[2,40,128]{2,1,0:T(8,128)S(1)}, f32[8,2,8,8,128]{4,3,2,1,0:T(8,128)S(1)}, f32[8,2,8,8,128]{4,3,2,1,0:T(8,128)S(1)}) custom-call(f32[2,8,8,8,128]{4,3,2,1,0:T(8,128)} %bitcast.4, f32[8,128]{1,0:T(8,128)} %refs_1_.1, f32[2,8,128]{2,1,0:T(8,128)} %refs_2_.1, s32[2,1,8,16]{3,2,1,0:T(8,128)} %bitcast.5, f32[2,1,8,16]{3,2,1,0:T(8,128)} %bitcast.6, ...), custom_call_target="tpu_custom_call" | custom-call | tf_op jit(solution)/shard_map/pallas_call | solution.py:751
  58.1 4.9 %shard_map.65 = f32[2,64,8,128]{3,2,1,0:T(8,128)} custom-call(f32[2,40,128]{2,1,0:T(8,128)S(1)} %get-tuple-element.8.gx, f32[8,2,8,8,128]{4,3,2,1,0:T(8,128)S(1)} %get-tuple-element.9.own, f32[8,2,8,8,128]{4,3,2,1,0:T(8,128)S(1)} %get-tuple-element.10.other), custom_call_target="tpu_custom_call" | custom-call | tf_op jit(solution)/shard_map/pallas_call | solution.py:778

commit v3 on v2

--- a/solution.py
+++ b/solution.py
@@ -137,20 +137,51 @@
 VMEM = pltpu.VMEM
 EDGE = 16
 SUB = 8
-CHUNK = 4
+CHUNK = 2
 VMEM_LIMIT = 40 * 2**20
 
 
+def segment_of(shape, tiles):
+    lane = lax.broadcasted_iota(jnp.int32, shape, len(shape) - 1)
+    width = shape[-1] // tiles
+    return lax.rem(lane + width // 2, shape[-1]) // width
+
+
 def east(field):
-    width, axis = (field.shape[-1], field.ndim - 1)
-    return pltpu.roll(field, width - 1, axis) - pltpu.roll(field, 1, axis)
-
-
-def north(field, first_row, last_row):
-    height = field.shape[0]
-    after = jnp.where(last_row, 0.0, pltpu.roll(field, height - 1, 0))
-    before = jnp.where(first_row, 0.0, pltpu.roll(field, 1, 0))
-    return after - before
+    tiles, cols = (field.shape[1] - 1, field.shape[3])
+    width = cols // tiles
+    lane = lax.broadcasted_iota(jnp.int32, field.shape[2:], 1)
+
+    def moved(shift, seam):
+        turned = pltpu.roll(field, shift % cols, 3)
+        halo = turned[:, tiles]
+        parts = []
+        for a in range(tiles):
+            here = lane == (a * width + seam) % cols
+            parts.append(jnp.where(here, turned[:, tiles], turned[:, a]))
+            halo = jnp.where(here, turned[:, a], halo)
+        return parts + [halo]
+
+    return jnp.stack(
+        [after - before for after, before in zip(moved(-1, -1), moved(1, 0))], axis=1
+    )
+
+
+def set_edges(ref):
+    tiles, cols = (ref.shape[1] - 1, ref.shape[3])
+    width = cols // tiles
+    segment = segment_of(ref.shape[2:], tiles)
+    zero = jnp.zeros(ref.shape[2:], jnp.float32)
+    first, last = (1, ref.shape[0] - 2)
+    for a in range(tiles):
+        ref[0, a] = pltpu.roll(ref[last, a - 1], width, 1) if a else zero
+        ref[last + 1, a] = (
+            pltpu.roll(ref[first, a + 1], cols - width, 1) if a + 1 < tiles else zero
+        )
+    ref[0, tiles] = jnp.where(segment == 0, 0.0, pltpu.roll(ref[last, tiles], width, 1))
+    ref[last + 1, tiles] = jnp.where(
+        segment == tiles - 1, 0.0, pltpu.roll(ref[first, tiles], cols - width, 1)
+    )
 
 
 def flat_lines(blocks, width):
@@ -173,14 +204,6 @@
     return lines
 
 
-def each(start, count, body):
-    def step(i, carry):
-        body(i)
-        return carry
-
-    lax.fori_loop(start, count, step, 0)
-
-
 def send(src, dst, send_sem, recv_sem, device):
     return pltpu.make_async_remote_copy(
         src_ref=src,
@@ -211,19 +234,30 @@
 
     for n in range(len(chunks)):
         height[inner[n]] = start[0, chunks[n]] + got[k, 1, chunks[n]]
+    set_edges(height)
     for n in range(len(chunks)):
         keep = 1.0 - got[k, 0, chunks[n]]
         got[k, 0, chunks[n]] = keep
         new_speeds(n, keep, start[1, chunks[n]], start[2, chunks[n]])
+    set_edges(speed_n)
 
     def middle(step, carry):
         new_height()
+        set_edges(height)
         for n in range(len(chunks)):
             new_speeds(n, got[k, 0, chunks[n]], speed_e[chunks[n]], speed_n[inner[n]])
+        set_edges(speed_n)
         return carry
 
     lax.fori_loop(1, STEPS - 1, middle, 0)
-    new_height()
+    tiles = start.shape[2] - 1
+    for n in range(len(chunks)):
+        flow = east(speed_e[chunks[n]])[:, 0:tiles] + (
+            speed_n[upper[n], 0:tiles] - speed_n[chunks[n], 0:tiles]
+        )
+        height[inner[n], 0:tiles] = (
+            height[inner[n], 0:tiles] - depth_step * flow + got[k, 1, chunks[n], 0:tiles]
+        )
 
 
 def inverse_below(matrix):
@@ -372,19 +406,17 @@
     owns, others, gxs, aux, lin, fin, slots_here, values_here, precision_here = refs[9:18]
     cells, info, start, height, speed_e, speed_n = refs[18:24]
     gots, edges, goths, outgoing, arriveds, part, partner_parts, half_sum, halves_all = refs[24:33]
-    load, send_a, recv_a, send_l, recv_l, send_p, recv_p, send_h, recv_h = refs[33:42]
-    send_o, recv_o, send_y, recv_y, send_x, recv_x, send_z, recv_z = refs[42:]
+    load, send_a, recv_a, send_p, recv_p, send_h, recv_h = refs[33:40]
+    send_y, recv_y, send_x, recv_x = refs[40:]
     lat, lon, ens = (lax.axis_index("lat"), lax.axis_index("lon"), lax.axis_index("ens"))
     blocks = n_lat * n_lon
     me = lat * n_lon + lon
     column = n_lat * n_ens
     here = ens * n_lat + lat
     groups, _, rows, _, cols = own_out.shape
-    all_rows = n_lat * rows
     groups_here = groups // n_lat
     share = n_lat // n_ens
     lane = lax.broadcasted_iota(jnp.int32, (SUB, cols), 1)
-    own_rows = pl.ds(lat * rows, rows)
 
     def at(lat_to, lon_to, ens_to):
         return {"lat": lat_to, "lon": lon_to, "ens": ens_to}
@@ -404,8 +436,13 @@
     def greet(device):
         pl.semaphore_signal(barrier, inc=1, device_id=device, device_id_type=MESH)
 
-    each(1, blocks, lambda i: greet(same_core(lax.rem(me + i, blocks))))
-    each(0, n_lat, lambda i: greet(at(i, lon, 1 - ens)))
+    for i in range(1, blocks):
+        greet(same_core(lax.rem(me + i, blocks)))
+    for i in range(n_lat):
+        greet(at(i, lon, 1 - ens))
+
+    def landed(ref, sem):
+        pltpu.make_async_copy(ref, ref, sem).wait()
 
     small = [
         pltpu.make_async_copy(src, dst, load.at[n])
@@ -419,19 +456,13 @@
             )
         )
     ]
-    large = [
-        pltpu.make_async_copy(
-            params.at[p, :, :, r, :], owns.at[0, :, p, r], load.at[len(small) + p * rows + r]
-        )
-        for p in range(2)
-        for r in range(rows)
-    ]
-    for copy in small + large:
+    for copy in small:
         copy.start()
-    zero_row = jnp.zeros((1, SUB, 2 * cols), jnp.float32)
-    for ref in (height, speed_n):
-        ref[0:1] = zero_row
-        ref[all_rows + 1 : all_rows + 2] = zero_row
+    for p in range(2):
+        for r in range(rows):
+            pltpu.make_async_copy(
+                params.at[p, :, :, r, :], owns.at[0, :, p, r], load.at[len(small)]
+            ).start()
     info[...] = jnp.zeros(info.shape, jnp.float32)
     for copy in small:
         copy.wait()
@@ -445,15 +476,14 @@
     )
     lines.append(jnp.zeros((rows - len(lines), cols), jnp.float32))
     aux[3] = jnp.concatenate(lines, axis=0)
-    for copy in large:
-        copy.wait()
+    landed(owns.at[0], load.at[len(small)])
 
     def field_copy(i, d):
         return send(
             aux.at[0:3],
-            fin.at[d % 3, lat],
-            send_a.at[i, d % 3],
-            recv_a.at[i, d % 3],
+            fin.at[(d % 3) * n_lat + lat],
+            send_a.at[0],
+            recv_a.at[0],
             at(lax.rem(lat + i, n_lat), east_of(-d), ens),
         )
 
@@ -461,8 +491,8 @@
         return send(
             aux.at[3],
             lin.at[me],
-            send_l.at[i],
-            recv_l.at[i],
+            send_a.at[1],
+            recv_a.at[1],
             same_core(lax.rem(me + i, blocks)),
         )
 
@@ -474,9 +504,9 @@
             to = lax.rem(lat + i, n_lat)
             return send(
                 own.at[to * groups_here + k],
-                got.at[k, :, own_rows, :, pl.ds(0, cols)],
-                send_p.at[t, k, i],
-                recv_p.at[t, k, i],
+                got.at[k, :, :, lat],
+                send_p.at[k],
+                recv_p.at[k],
                 at(to, lon, ens),
             )
 
@@ -485,72 +515,78 @@
             return send(
                 edges.at[side, to * groups_here + k],
                 goth.at[k, lat, side],
-                send_h.at[t, k, i, side],
-                recv_h.at[t, k, i, side],
+                send_h.at[k],
+                recv_h.at[k],
                 at(to, east_of(2 * side - 1), ens),
             )
 
-        swap = send(own, other, send_o.at[t], recv_o.at[t], partner)
+        swap = send(own, other, send_x.at[t, 0], recv_x.at[t, 0], partner)
 
         def pack_edges(g):
+            slot = lane // EDGE
             for p in range(2):
                 left = jnp.zeros((SUB, cols), jnp.float32)
                 right = left
                 for r in range(rows):
-                    tile = own[g, p, r]
-                    here_lanes = lane // EDGE == r
-                    left = jnp.where(here_lanes, pltpu.roll(tile, EDGE * r, 1), left)
-                    shift = (EDGE * r + EDGE) % cols
-                    right = jnp.where(here_lanes, pltpu.roll(tile, shift, 1), right)
-                edges[0, g, p] = left
-                edges[1, g, p] = right
+                    tile = pltpu.roll(own[g, p, r], EDGE * r, 1)
+                    left = jnp.where(slot == r, tile, left)
+                    right = jnp.where(slot == (r + rows - 1) % rows, tile, right)
+                edges[0, g, p] = pltpu.roll(left, 2 * EDGE * lat, 1)
+                edges[1, g, p] = pltpu.roll(right, 2 * EDGE * lat, 1)
 
         if t == 0:
             for g in range(groups):
                 pack_edges(g)
             pl.semaphore_wait(barrier, blocks - 1 + n_lat)
-            each(1, n_lat, lambda i: field_copy(i, 0).start())
-            for d in (1, -1):
-                each(0, n_lat, lambda i: field_copy(i, d).start())
+            for d in (0, 1, -1):
+                for i in range(0 if d else 1, n_lat):
+                    field_copy(i, d).start()
         for k in range(groups_here):
-            each(1, n_lat, lambda i: param_copy(k, i).start())
+            for i in range(1, n_lat):
+                param_copy(k, i).start()
             if t and k == 0:
                 for g in range(groups):
                     pack_edges(g)
             for side in range(2):
-                each(0, n_lat, lambda i: edge_copy(k, i, side).start())
+                for i in range(n_lat):
+                    edge_copy(k, i, side).start()
             if t == 0 and k == 0:
-                each(1, blocks, lambda i: line_copy(i).start())
+                for i in range(1, blocks):
+                    line_copy(i).start()
         swap.start()
         for k in range(groups_here):
-            got[k, :, own_rows, :, 0:cols] = own[lat * groups_here + k]
+            got[k, :, :, pl.ds(lat, 1)] = own[pl.ds(lat * groups_here + k, 1)].reshape(
+                2, rows, 1, SUB, cols
+            )
 
         if t == 0:
+            fin[pl.ds(lat, 1)] = aux[0:3].reshape(1, 3, rows, cols)
+            lin[pl.ds(me, 1)] = aux[3:4]
+            landed(fin.at[0 : 3 * n_lat - 1], recv_a.at[0])
+            segment = segment_of((rows, cols), n_lat)
+            inside = lax.rem(lane + EDGE, 2 * EDGE) < EDGE
             for i in range(3):
-                fin[0, pl.ds(lat, 1), i] = aux[i : i + 1]
-            lin[pl.ds(me, 1)] = aux[3:4]
-            each(1, n_lat, lambda i: field_copy(i, 0).wait())
-            for d in (1, -1):
-                each(0, n_lat, lambda i: field_copy(i, d).wait())
-
-            def whole(i):
-                lines = []
+                halo = jnp.zeros((rows, cols), jnp.float32)
+                tiles = []
                 for a in range(n_lat):
-                    after, before = (fin[1, a, i], fin[2, a, i])
-                    outer = jnp.where(
-                        lane < EDGE, after, jnp.where(lane >= cols - EDGE, before, 0.0)
-                    )
-                    lines.append(jnp.concatenate([fin[0, a, i], outer], axis=1))
-                return jnp.concatenate(lines, axis=0)
-
-            row_ids = lax.broadcasted_iota(jnp.int32, (all_rows, 2 * cols), 0)
-            first_row, last_row = (row_ids == 0, row_ids == all_rows - 1)
-            speed_e0, speed_n0 = (whole(1), whole(2))
-            flow = east(speed_e0) + north(speed_n0, first_row, last_row)
-            for i, field in enumerate((whole(0) - depth_step * flow, speed_e0, speed_n0)):
-                for r in range(all_rows):
-                    start[i, r] = jnp.broadcast_to(field[r : r + 1], (SUB, 2 * cols))
-            each(1, blocks, lambda i: line_copy(i).wait())
+                    turned = [
+                        pltpu.roll(fin[d * n_lat + a, i], 2 * EDGE * a, 1) for d in range(3)
+                    ]
+                    tiles.append(turned[0])
+                    outer = jnp.where(inside, turned[2], turned[1])
+                    halo = jnp.where(segment == a, outer, halo)
+                for a, tile in enumerate(tiles + [halo]):
+                    for r in range(rows):
+                        start[i, r, a] = jnp.broadcast_to(tile[r : r + 1], (SUB, cols))
+            for r in range(rows):
+                speed_n[r + 1] = start[2, r]
+            set_edges(speed_n)
+            for r in range(0, rows, CHUNK):
+                flow = east(start[1, r : r + CHUNK]) + (
+                    speed_n[r + 2 : r + 2 + CHUNK] - speed_n[r : r + CHUNK]
+                )
+                start[0, r : r + CHUNK] = start[0, r : r + CHUNK] - depth_step * flow
+            landed(lin.at[0 : blocks - 1], recv_a.at[1])
             for n in range(ITERS):
                 for a in range(n_lat):
                     line = lin[a * n_lon + lon][n : n + 1].astype(jnp.int32)
@@ -562,38 +598,41 @@
             return send(
                 outgoing.at[pl.ds((to // n_lat) * share, share), part_rows],
                 arrived.at[:, here, part_rows],
-                send_y.at[t, k, i],
-                recv_y.at[t, k, i],
+                send_y.at[k],
+                recv_y.at[k],
                 same_column(to),
             )
 
         def group(k, carry):
-            each(1, n_lat, lambda i: param_copy(k, i).wait())
-            for side in range(2):
-                each(0, n_lat, lambda i: edge_copy(k, i, side).wait())
-            for a in range(n_lat):
-                for p in range(2):
-                    after, before = (goth[k, a, 0, p], goth[k, a, 1, p])
-                    for r in range(rows):
-                        shift = (cols - EDGE * r) % cols
-                        right = pltpu.roll(after, shift, 1)
-                        left = pltpu.roll(before, (shift + cols - EDGE) % cols, 1)
-                        got[k, p, a * rows + r, :, cols : 2 * cols] = jnp.where(
-                            lane < EDGE, right, jnp.where(lane >= cols - EDGE, left, 0.0)
-                        )
+            landed(got.at[k, :, :, 0 : n_lat - 1], recv_p.at[k])
+            for p in range(2):
+                for r in range(rows):
+                    for a in range(1, n_lat):
+                        got[k, p, r, a] = pltpu.roll(got[k, p, r, a], 2 * EDGE * a, 1)
+            landed(goth.at[k], recv_h.at[k])
+            slot = lane // EDGE
+            for p in range(2):
+                for r in range(rows):
+                    halo = jnp.zeros((SUB, cols), jnp.float32)
+                    for a in range(n_lat):
+                        after, before = (goth[k, a, 0, p], goth[k, a, 1, p])
+                        halo = jnp.where(slot == (2 * a + r) % rows, after, halo)
+                        halo = jnp.where(slot == (2 * a + r + rows - 1) % rows, before, halo)
+                    got[k, p, r, n_lat] = pltpu.roll(halo, (cols - EDGE * r) % cols, 1)
             run_group(k, got, start, height, speed_e, speed_n)
             for a in range(n_lat):
                 line = t * n_lat + a
                 wanted = jnp.broadcast_to(cells[line : line + 1], (SUB, cols))
-                lanes = jnp.bitwise_and(wanted, cols - 1)
+                lanes = jnp.bitwise_and(wanted + 2 * EDGE * a, cols - 1)
                 where_row = jnp.right_shift(wanted, cols.bit_length() - 1)
                 found = jnp.zeros((SUB, cols), jnp.float32)
                 for r in range(rows):
-                    tile = height[a * rows + r + 1, :, 0:cols]
+                    tile = height[r + 1, a]
                     picked = jnp.take_along_axis(tile, lanes, axis=1)
                     found = jnp.where(where_row == r, picked, found)
                 outgoing[a, pl.ds(k * SUB, SUB)] = found
-            each(1, column, lambda i: answer_copy(k, i).start())
+            for i in range(1, column):
+                answer_copy(k, i).start()
             return carry
 
         lax.fori_loop(0, groups_here, group, 0)
@@ -623,7 +662,7 @@
                         jnp.where(wanted, spread_out, 0.0), axis=0, keepdims=True
                     )
         for k in range(groups_here):
-            each(1, column, lambda i: answer_copy(k, i).wait())
+            landed(arrived.at[:, 0 : column - 1, k * SUB : (k + 1) * SUB], recv_y.at[k])
 
         members = column * arrived.shape[2]
         predicted = jnp.concatenate(
@@ -650,7 +689,7 @@
         for e, piece in enumerate(packed_halves(product, n_ens)):
             part[e] = piece
 
-        trade = send(part.at[1 - ens], partner_part, send_x.at[t, 0], recv_x.at[t, 0], partner)
+        trade = send(part.at[1 - ens], partner_part, send_x.at[t, 1], recv_x.at[t, 1], partner)
         trade.start()
         trade.wait()
         half_sum[...] = part[ens] + partner_part[...]
@@ -659,22 +698,31 @@
             return send(
                 half_sum,
                 halves.at[lon],
-                send_z.at[t, i],
-                recv_z.at[t, i],
+                send_x.at[t, 3],
+                recv_x.at[t, 3],
                 at(lat, east_of(i), ens),
             )
 
-        each(1, n_lon, lambda i: half_copy(i).start())
+        for i in range(1, n_lon):
+            half_copy(i).start()
         halves[lon] = half_sum[...]
-        each(1, n_lon, lambda i: half_copy(i).wait())
+        landed(halves.at[0 : n_lon - 1], recv_x.at[t, 3])
+        landed(halves.at[0 : n_lon - 1], send_x.at[t, 3])
         total = halves[0]
         for b in range(1, n_lon):
             total = total + halves[b]
         half_sum[...] = total
-        finish = send(half_sum, gx.at[ens], send_x.at[t, 1], recv_x.at[t, 1], partner)
+        finish = send(half_sum, gx.at[ens], send_x.at[t, 2], recv_x.at[t, 2], partner)
         finish.start()
         gx[ens] = total
         swap.wait()
+        for k in range(groups_here):
+            landed(got.at[k, :, :, 0 : n_lat - 1], send_p.at[k])
+            landed(goth.at[k], send_h.at[k])
+            landed(arrived.at[:, 0 : column - 1, k * SUB : (k + 1) * SUB], send_y.at[k])
+        if t == 0:
+            landed(fin.at[0 : 3 * n_lat - 1], send_a.at[0])
+            landed(lin.at[0 : blocks - 1], send_a.at[1])
         finish.wait()
 
     for t in range(ITERS):
@@ -700,7 +748,6 @@
     groups_here = groups // n_lat
     members = groups * SUB * n_ens
     share = n_lat // n_ens
-    all_rows = n_lat * rows
     lines = members // 2 // n_ens + SUB
     f32 = jnp.float32
     dma = pltpu.SemaphoreType.DMA
@@ -716,17 +763,17 @@
         VMEM((max(ITERS - 1, 1),) + gx_shape, f32),
         VMEM((4, rows, cols), f32),
         VMEM((blocks, rows, cols), f32),
-        VMEM((3, n_lat, 3, rows, cols), f32),
+        VMEM((3 * n_lat, 3, rows, cols), f32),
     ]
     scratch += [VMEM(obs.shape, obs.dtype) for obs in operands[3:]]
     scratch += [
         VMEM((ITERS * n_lat, cols), jnp.int32),
         VMEM((SUB, share * cols), f32),
-        VMEM((3, all_rows, SUB, 2 * cols), f32),
-        VMEM((all_rows + 2, SUB, 2 * cols), f32),
-        VMEM((all_rows, SUB, 2 * cols), f32),
-        VMEM((all_rows + 2, SUB, 2 * cols), f32),
-        VMEM((ITERS, groups_here, 2, all_rows, SUB, 2 * cols), f32),
+        VMEM((3, rows, n_lat + 1, SUB, cols), f32),
+        VMEM((rows + 2, n_lat + 1, SUB, cols), f32),
+        VMEM((rows, n_lat + 1, SUB, cols), f32),
+        VMEM((rows + 2, n_lat + 1, SUB, cols), f32),
+        VMEM((ITERS, groups_here, 2, rows, n_lat + 1, SUB, cols), f32),
         VMEM((2, groups, 2, SUB, cols), f32),
         VMEM((ITERS, groups_here, n_lat, 2, 2, SUB, cols), f32),
         VMEM((n_lat, groups_here * SUB, cols), f32),
@@ -735,18 +782,9 @@
         VMEM((ITERS, lines, members), f32),
         VMEM((lines, members), f32),
         VMEM((ITERS, n_lon, lines, members), f32),
-        dma((5 + 2 * rows,)),
+        dma((6,)),
     ]
-    for shape in (
-        (n_lat, 3),
-        (blocks,),
-        (ITERS, groups_here, n_lat),
-        (ITERS, groups_here, n_lat, 2),
-        (ITERS,),
-        (ITERS, groups_here, column),
-        (ITERS, 2),
-        (ITERS, n_lon),
-    ):
+    for shape in ((2,), (groups_here,), (groups_here,), (groups_here,), (ITERS, 4)):
         scratch += both(shape)
     return pl.pallas_call(
         functools.partial(ensemble_kernel, n_lat, n_lon, n_ens),
@@ -808,6 +846,7 @@
         and members_here * n_ens == cols
         and cols == 128
         and EDGE * rows == cols
+        and 2 * EDGE * n_lat == cols
         and 2 * STEPS <= EDGE
         and ITERS * 3 <= rows
         and obs_slots.shape[2] * obs_slots.shape[3] == cols

time: 63.2 us -> 60 us (0.949)
  Pallas kernels: 63 us -> 59.8 us
    pallas_call x1, Pallas kernels: 58.1 us -> 54.9 us  [ensemble_call(): pl.pallas_call(functools.partial(ensemble_kernel, n_lat, n_lon, n_ens), o...]
where the time goes in v3:
time: 60 us; the launch traced here: 59.8 us
  Pallas kernels  59.8 us (100%)
    pallas_call x1, Pallas kernels, ensemble_call(): pl.pallas_call(functools.partial(ensemble_kernel, n_lat, n_lon, n_ens), o...  54.9 us
    pallas_call x1, Pallas kernels, update_call(): pl.pallas_call(update_kernel, out_shape=jax.ShapeDtypeStruct(shape, jnp.f...  4.86 us

profile of v3, /device:TPU:0, one launch (start us, length us, event | category | flops | bytes accessed | tf_op | source)
XLA Modules:
  0.0 59.8 jit_solution(15854246701293414618)
XLA Ops:
  0.0 54.9 %shard_map.64 = (f32[2,40,128]{2,1,0:T(8,128)S(1)}, f32[8,2,8,8,128]{4,3,2,1,0:T(8,128)S(1)}, f32[8,2,8,8,128]{4,3,2,1,0:T(8,128)S(1)}) custom-call(f32[2,8,8,8,128]{4,3,2,1,0:T(8,128)} %bitcast.4, f32[8,128]{1,0:T(8,128)} %refs_1_.1, f32[2,8,128]{2,1,0:T(8,128)} %refs_2_.1, s32[2,1,8,16]{3,2,1,0:T(8,128)} %bitcast.5, f32[2,1,8,16]{3,2,1,0:T(8,128)} %bitcast.6, ...), custom_call_target="tpu_custom_call" | custom-call | tf_op jit(solution)/shard_map/pallas_call | solution.py:789
  54.9 4.9 %shard_map.65 = f32[2,64,8,128]{3,2,1,0:T(8,128)} custom-call(f32[2,40,128]{2,1,0:T(8,128)S(1)} %get-tuple-element.8.gx, f32[8,2,8,8,128]{4,3,2,1,0:T(8,128)S(1)} %get-tuple-element.9.own, f32[8,2,8,8,128]{4,3,2,1,0:T(8,128)S(1)} %get-tuple-element.10.other), custom_call_target="tpu_custom_call" | custom-call | tf_op jit(solution)/shard_map/pallas_call | solution.py:816

commit v4 on v3

--- a/solution.py
+++ b/solution.py
@@ -260,7 +260,7 @@
         )
 
 
-def inverse_below(matrix):
+def inverse_rows(matrix):
     size = matrix.shape[1]
     strip = size // 2 // SUB
     row_ids = lax.broadcasted_iota(jnp.int32, (SUB, size), 0)
@@ -281,7 +281,8 @@
         return tile
 
     for base in range(0, size // SUB, strip):
-        inner = tiles[base : base + strip]
+        last = base + strip == size // SUB
+        inner = tiles[base:] if last else tiles[base : base + strip]
         columns = columns_of(inner[0], base * SUB)
         for n in range(strip):
             start = (base + n) * SUB
@@ -316,10 +317,12 @@
                         value - below[k] * line[k : k + 1] for value, line in zip(later, ahead)
                     ]
                 columns = later
-            for m in range(strip):
+            for m in range(len(inner)):
                 if m != n and not (follows and m == n + 1):
                     after[m] = less_rows(inner[m], band, columns_of(inner[m], start), rows)
             inner = after
+        if last:
+            return inner[:strip], inner[strip]
         outer = [m for m in range(len(tiles)) if not base <= m < base + strip]
         lines = [
             inner[m - base] if base <= m < base + strip else zero for m in range(size // SUB)
@@ -334,51 +337,55 @@
         for n, m in enumerate(outer):
             tiles[m] = jnp.where(band, 0.0, tiles[m]) - product[n * SUB : (n + 1) * SUB]
         tiles[base : base + strip] = inner
-    return jnp.concatenate(tiles, axis=0)
-
-
-def packed_halves(product, n_ens):
-    half = product.shape[1] // 2
-    row_ids = lax.broadcasted_iota(jnp.int32, (half, 2 * half), 0)
-    lane_ids = lax.broadcasted_iota(jnp.int32, (half, 2 * half), 1)
-    top, bottom = (product[0:half], product[half : 2 * half])
+
+
+def packed(e, rows, tail):
+    lines, width = (rows.shape[0] // 2, rows.shape[1])
+    half = width // 2
+    row_ids = lax.broadcasted_iota(jnp.int32, (lines, width), 0) + e * lines
+    lane_ids = lax.broadcasted_iota(jnp.int32, (lines, width), 1)
+    top, bottom = (rows[:lines], rows[lines:])
     dense = jnp.where(lane_ids <= row_ids + half, bottom, pltpu.roll(top, half, 1))
     diagonal = jnp.sum(jnp.where(lane_ids == row_ids, top, 0.0), axis=0, keepdims=True)
-    tail = jnp.where(row_ids[0:SUB] == 1, diagonal, product[2 * half :])
-    lines = half // n_ens
-    return [
-        jnp.concatenate([dense[e * lines : (e + 1) * lines], tail], axis=0)
-        for e in range(n_ens)
-    ]
+    tail_ids = lax.broadcasted_iota(jnp.int32, tail.shape, 0)
+    return jnp.concatenate([dense, jnp.where(tail_ids == 1, diagonal, tail)], axis=0)
 
 
 def unpacked(parts):
     half = sum(part.shape[0] - SUB for part in parts)
     dense = jnp.concatenate([part[: part.shape[0] - SUB] for part in parts], axis=0)
-    tail = parts[0][parts[0].shape[0] - SUB :]
+    tails = [part[part.shape[0] - SUB :] for part in parts]
+    diagonal = sum(tail[1:2] for tail in tails)
     row_ids = lax.broadcasted_iota(jnp.int32, (half, 2 * half), 0)
     lane_ids = lax.broadcasted_iota(jnp.int32, (half, 2 * half), 1)
     turned = jnp.concatenate([dense, dense], axis=0).T
     upper = jnp.where(lane_ids > row_ids, pltpu.roll(dense, half, 1), turned[half:])
-    upper = jnp.where(lane_ids == row_ids, tail[1:2], upper)
+    upper = jnp.where(lane_ids == row_ids, diagonal, upper)
     top = jnp.where(lane_ids >= half, turned[:half], upper)
     bottom = jnp.where(lane_ids <= row_ids + half, dense, turned[half:])
-    return jnp.concatenate([top, bottom], axis=0), tail[0:1]
+    return top, bottom, tails[0][0:1]
 
 
 def member_weights(gx, ens):
     members = gx.shape[2]
     half = members // 2
-    gram, line = unpacked([gx[e] for e in range(gx.shape[0])])
-    ids = [lax.broadcasted_iota(jnp.int32, gram.shape, axis) for axis in (0, 1)]
-    unit = (ids[0] == ids[1]).astype(jnp.float32)
+    top, bottom, line = unpacked([gx[e] for e in range(gx.shape[0])])
+
+    def turned(value):
+        return pltpu.roll(value, half, 1)
+
+    swap = ens == 0
     line = jnp.broadcast_to(line, (SUB, members))
-    swept = inverse_below(jnp.concatenate([gram / members + unit, line], axis=0))
-    shift = swept[members : members + 1] / members
-    weights = swept[:members] - unit - shift
-    centred = weights - jnp.sum(weights, axis=1, keepdims=True) / members
-    mine = jnp.where(ens == 0, centred[:half], centred[half:])
-    return jnp.where(ens == 0, mine, pltpu.roll(mine, half, 1))
+    line = jnp.where(swap, turned(line), line)
+    upper = jnp.where(swap, turned(bottom), top) / members
+    lower = jnp.where(swap, turned(top), bottom) / members
+    row_ids = lax.broadcasted_iota(jnp.int32, (half, members), 0)
+    lane_ids = lax.broadcasted_iota(jnp.int32, (half, members), 1)
+    unit = (lane_ids == row_ids + half).astype(jnp.float32)
+    upper = upper + (lane_ids == row_ids).astype(jnp.float32)
+    rows, below = inverse_rows(jnp.concatenate([upper, lower + unit, line], axis=0))
+    weights = jnp.concatenate(rows, axis=0) - unit - below[0:1] / members
+    return weights - jnp.sum(weights, axis=1, keepdims=True) / members
 
 
 def updated_rows(mine, own, other, store):
@@ -389,7 +396,7 @@
             for q in (r, r + 1):
                 local.append(jnp.concatenate([own[g, p, q] for g in range(groups)], axis=0))
                 remote = [other[g, p, q] for g in range(groups)]
-                pair.append(jnp.concatenate([local[-1]] + remote, axis=0))
+                pair.append(jnp.concatenate(remote + [local[-1]], axis=0))
             added = jnp.dot(
                 mine,
                 jnp.concatenate(pair, axis=1),
@@ -679,20 +686,30 @@
         weighted = spread * precision
         extra = lax.broadcasted_iota(jnp.int32, (SUB, share * cols), 0) == 0
         extra = jnp.where(extra, jnp.broadcast_to(observed - centre, extra.shape), 0.0)
-        product = lax.dot_general(
-            jnp.concatenate([spread, extra], axis=0),
-            weighted,
-            (((1,), (1,)), ((), ())),
-            precision=lax.Precision.HIGHEST,
-            preferred_element_type=jnp.float32,
-        )
-        for e, piece in enumerate(packed_halves(product, n_ens)):
-            part[e] = piece
-
-        trade = send(part.at[1 - ens], partner_part, send_x.at[t, 1], recv_x.at[t, 1], partner)
+
+        def products(rows):
+            return lax.dot_general(
+                rows,
+                weighted,
+                (((1,), (1,)), ((), ())),
+                precision=lax.Precision.HIGHEST,
+                preferred_element_type=jnp.float32,
+            )
+
+        lines = members // 2 // n_ens
+        quarters = [spread[n * lines : (n + 1) * lines] for n in range(2 * n_ens)]
+        by_core = [
+            jnp.concatenate([quarters[e], quarters[n_ens + e]], axis=0) for e in range(n_ens)
+        ]
+        theirs = jnp.where(ens == 0, by_core[1], by_core[0])
+        product = products(jnp.concatenate([theirs, extra], axis=0))
+        tail = product[2 * lines :]
+        part[...] = packed(1 - ens, product[: 2 * lines], tail)
+        trade = send(part, partner_part, send_x.at[t, 1], recv_x.at[t, 1], partner)
         trade.start()
+        mine = packed(ens, products(jnp.where(ens == 0, by_core[0], by_core[1])), tail)
         trade.wait()
-        half_sum[...] = part[ens] + partner_part[...]
+        half_sum[...] = mine + partner_part[...]
 
         def half_copy(i):
             return send(
@@ -778,7 +795,7 @@
         VMEM((ITERS, groups_here, n_lat, 2, 2, SUB, cols), f32),
         VMEM((n_lat, groups_here * SUB, cols), f32),
         VMEM((ITERS, share, column, groups_here * SUB, cols), f32),
-        VMEM(gx_shape, f32),
+        VMEM(gx_shape[1:], f32),
         VMEM((ITERS, lines, members), f32),
         VMEM((lines, members), f32),
         VMEM((ITERS, n_lon, lines, members), f32),

time: 60 us -> 59.2 us (0.987)
  Pallas kernels: 59.8 us -> 59 us
where the time goes in v4:
time: 59.2 us; the launch traced here: 59 us
  Pallas kernels  59 us (100%)
    pallas_call x1, Pallas kernels, ensemble_call(): pl.pallas_call(functools.partial(ensemble_kernel, n_lat, n_lon, n_ens), o...  54.6 us
    pallas_call x1, Pallas kernels, update_call(): pl.pallas_call(update_kernel, out_shape=jax.ShapeDtypeStruct(shape, jnp.f...  4.44 us

profile of v4, /device:TPU:0, one launch (start us, length us, event | category | flops | bytes accessed | tf_op | source)
XLA Modules:
  0.0 59.0 jit_solution(8363651399607086766)
XLA Ops:
  0.0 54.6 %shard_map.64 = (f32[2,40,128]{2,1,0:T(8,128)S(1)}, f32[8,2,8,8,128]{4,3,2,1,0:T(8,128)S(1)}, f32[8,2,8,8,128]{4,3,2,1,0:T(8,128)S(1)}) custom-call(f32[2,8,8,8,128]{4,3,2,1,0:T(8,128)} %bitcast.4, f32[8,128]{1,0:T(8,128)} %refs_1_.1, f32[2,8,128]{2,1,0:T(8,128)} %refs_2_.1, s32[2,1,8,16]{3,2,1,0:T(8,128)} %bitcast.5, f32[2,1,8,16]{3,2,1,0:T(8,128)} %bitcast.6, ...), custom_call_target="tpu_custom_call" | custom-call | tf_op jit(solution)/shard_map/pallas_call | solution.py:806
  54.6 4.4 %shard_map.65 = f32[2,64,8,128]{3,2,1,0:T(8,128)} custom-call(f32[2,40,128]{2,1,0:T(8,128)S(1)} %get-tuple-element.8.gx, f32[8,2,8,8,128]{4,3,2,1,0:T(8,128)S(1)} %get-tuple-element.9.own, f32[8,2,8,8,128]{4,3,2,1,0:T(8,128)S(1)} %get-tuple-element.10.other), custom_call_target="tpu_custom_call" | custom-call | tf_op jit(solution)/shard_map/pallas_call | solution.py:833

commit v5 on v4

--- a/solution.py
+++ b/solution.py
@@ -137,6 +137,7 @@
 VMEM = pltpu.VMEM
 EDGE = 16
 SUB = 8
+AHEAD = 6
 CHUNK = 2
 VMEM_LIMIT = 40 * 2**20
 
@@ -292,9 +293,9 @@
             follows = n + 1 < strip
             ahead = []
             if follows:
-                ahead = columns_of(inner[n], start + SUB)
+                ahead = columns_of(inner[n], start + SUB)[:AHEAD]
                 below = columns_of(inner[n + 1], start)
-                later = columns_of(inner[n + 1], start + SUB)
+                later = columns_of(inner[n + 1], start + SUB)[:AHEAD]
             for k in range(SUB):
                 column = columns[k]
                 inverse = 1.0 / column[k : k + 1]
@@ -316,7 +317,7 @@
                     later = [
                         value - below[k] * line[k : k + 1] for value, line in zip(later, ahead)
                     ]
-                columns = later
+                columns = later + columns_of(after[n + 1], start + SUB)[AHEAD:]
             for m in range(len(inner)):
                 if m != n and not (follows and m == n + 1):
                     after[m] = less_rows(inner[m], band, columns_of(inner[m], start), rows)
@@ -411,6 +412,7 @@
     params, start_height, start_speed, slots_in, values_in, precision_in = refs[:6]
     gx_out, own_out, other_out = refs[6:9]
     owns, others, gxs, aux, lin, fin, slots_here, values_here, precision_here = refs[9:18]
+    outer_fields, refs = (refs[18], refs[:18] + refs[19:])
     cells, info, start, height, speed_e, speed_n = refs[18:24]
     gots, edges, goths, outgoing, arriveds, part, partner_parts, half_sum, halves_all = refs[24:33]
     load, send_a, recv_a, send_p, recv_p, send_h, recv_h = refs[33:40]
@@ -483,14 +485,23 @@
     )
     lines.append(jnp.zeros((rows - len(lines), cols), jnp.float32))
     aux[3] = jnp.concatenate(lines, axis=0)
+    slot = lane // EDGE
+    packed_fields = jnp.zeros((rows, cols), jnp.float32)
+    for i in range(3):
+        left = pltpu.roll(aux[i], EDGE * i, 1)
+        right = pltpu.roll(aux[i], (EDGE * (i + 5)) % cols, 1)
+        packed_fields = jnp.where(slot == i, left, packed_fields)
+        packed_fields = jnp.where(slot == i + 4, right, packed_fields)
+    aux[4] = packed_fields
     landed(owns.at[0], load.at[len(small)])
 
     def field_copy(i, d):
+        pick = 2 if d else 0
         return send(
-            aux.at[0:3],
-            fin.at[(d % 3) * n_lat + lat],
-            send_a.at[0],
-            recv_a.at[0],
+            aux.at[4] if d else aux.at[0:3],
+            outer_fields.at[(d % 3 - 1) * n_lat + lat] if d else fin.at[lat],
+            send_a.at[pick],
+            recv_a.at[pick],
             at(lax.rem(lat + i, n_lat), east_of(-d), ens),
         )
 
@@ -503,19 +514,19 @@
             same_core(lax.rem(me + i, blocks)),
         )
 
+    def param_copy(t, own, k, i, which):
+        to = lax.rem(lat + i, n_lat)
+        return send(
+            own.at[to * groups_here + k, which],
+            gots.at[t, k, which, :, lat],
+            send_p.at[k],
+            recv_p.at[k],
+            at(to, lon, ens),
+        )
+
     def run_iteration(t, own, other, gx):
         got, goth, arrived = (gots.at[t], goths.at[t], arriveds.at[t])
         partner_part, halves = (partner_parts.at[t], halves_all.at[t])
-
-        def param_copy(k, i):
-            to = lax.rem(lat + i, n_lat)
-            return send(
-                own.at[to * groups_here + k],
-                got.at[k, :, :, lat],
-                send_p.at[k],
-                recv_p.at[k],
-                at(to, lon, ens),
-            )
 
         def edge_copy(k, i, side):
             to = lax.rem(lat + i, n_lat)
@@ -550,7 +561,7 @@
                     field_copy(i, d).start()
         for k in range(groups_here):
             for i in range(1, n_lat):
-                param_copy(k, i).start()
+                param_copy(t, own, k, i, pl.ds(1, 1) if t and k == 0 else pl.ds(0, 2)).start()
             if t and k == 0:
                 for g in range(groups):
                     pack_edges(g)
@@ -569,18 +580,21 @@
         if t == 0:
             fin[pl.ds(lat, 1)] = aux[0:3].reshape(1, 3, rows, cols)
             lin[pl.ds(me, 1)] = aux[3:4]
-            landed(fin.at[0 : 3 * n_lat - 1], recv_a.at[0])
+            landed(fin.at[0 : n_lat - 1], recv_a.at[0])
+            landed(outer_fields, recv_a.at[2])
             segment = segment_of((rows, cols), n_lat)
             inside = lax.rem(lane + EDGE, 2 * EDGE) < EDGE
             for i in range(3):
                 halo = jnp.zeros((rows, cols), jnp.float32)
                 tiles = []
                 for a in range(n_lat):
-                    turned = [
-                        pltpu.roll(fin[d * n_lat + a, i], 2 * EDGE * a, 1) for d in range(3)
-                    ]
-                    tiles.append(turned[0])
-                    outer = jnp.where(inside, turned[2], turned[1])
+                    tiles.append(pltpu.roll(fin[a, i], 2 * EDGE * a, 1))
+                    shift = 2 * EDGE * a - EDGE * i
+                    after = pltpu.roll(outer_fields[a], shift % cols, 1)
+                    before = pltpu.roll(
+                        outer_fields[n_lat + a], (shift - 5 * EDGE) % cols, 1
+                    )
+                    outer = jnp.where(inside, before, after)
                     halo = jnp.where(segment == a, outer, halo)
                 for a, tile in enumerate(tiles + [halo]):
                     for r in range(rows):
@@ -738,7 +752,8 @@
             landed(goth.at[k], send_h.at[k])
             landed(arrived.at[:, 0 : column - 1, k * SUB : (k + 1) * SUB], send_y.at[k])
         if t == 0:
-            landed(fin.at[0 : 3 * n_lat - 1], send_a.at[0])
+            landed(fin.at[0 : n_lat - 1], send_a.at[0])
+            landed(outer_fields, send_a.at[2])
             landed(lin.at[0 : blocks - 1], send_a.at[1])
         finish.wait()
 
@@ -750,9 +765,12 @@
         if not last:
             new = own_out if t + 1 == ITERS - 1 else owns.at[t + 1]
 
-            def store(p, r, value, new=new):
+            def store(p, r, value, t=t + 1, new=new):
                 for g in range(groups):
                     new[g, p, r] = value[g * SUB : (g + 1) * SUB]
+                if p == 0 and r == rows - 1:
+                    for i in range(1, n_lat):
+                        param_copy(t, new, 0, i, pl.ds(0, 1)).start()
 
             updated_rows(member_weights(gx, ens), own, other, store)
 
@@ -778,11 +796,12 @@
         VMEM((max(ITERS - 1, 1),) + own_shape, f32),
         VMEM((max(ITERS - 1, 1),) + own_shape, f32),
         VMEM((max(ITERS - 1, 1),) + gx_shape, f32),
-        VMEM((4, rows, cols), f32),
+        VMEM((5, rows, cols), f32),
         VMEM((blocks, rows, cols), f32),
-        VMEM((3 * n_lat, 3, rows, cols), f32),
+        VMEM((n_lat, 3, rows, cols), f32),
     ]
     scratch += [VMEM(obs.shape, obs.dtype) for obs in operands[3:]]
+    scratch += [VMEM((2 * n_lat, rows, cols), f32)]
     scratch += [
         VMEM((ITERS * n_lat, cols), jnp.int32),
         VMEM((SUB, share * cols), f32),
@@ -801,7 +820,7 @@
         VMEM((ITERS, n_lon, lines, members), f32),
         dma((6,)),
     ]
-    for shape in ((2,), (groups_here,), (groups_here,), (groups_here,), (ITERS, 4)):
+    for shape in ((3,), (groups_here,), (groups_here,), (groups_here,), (ITERS, 4)):
         scratch += both(shape)
     return pl.pallas_call(
         functools.partial(ensemble_kernel, n_lat, n_lon, n_ens),
@@ -816,17 +835,13 @@
 
 
 def update_kernel(gx, own, other, out, new, sems):
-    copies = [pltpu.make_async_copy(new.at[p], out.at[p], sems.at[p]) for p in range(2)]
-    rows = own.shape[2]
-
     def store(p, r, value):
-        new[p, :, r, :] = value
-        if r == rows - 1:
-            copies[p].start()
+        new[p, r] = value
+        pltpu.make_async_copy(new.at[p, r], out.at[p, :, r, :], sems.at[p]).start()
 
     updated_rows(member_weights(gx, lax.axis_index("ens")), own, other, store)
-    for copy in copies:
-        copy.wait()
+    for p in range(2):
+        pltpu.make_async_copy(new.at[p], new.at[p], sems.at[p]).wait()
 
 
 def update_call(shape, *operands):
@@ -835,7 +850,10 @@
         out_shape=jax.ShapeDtypeStruct(shape, jnp.float32),
         in_specs=[pl.BlockSpec(memory_space=VMEM)] * len(operands),
         out_specs=pl.BlockSpec(memory_space=pltpu.HBM),
-        scratch_shapes=[VMEM(shape, jnp.float32), pltpu.SemaphoreType.DMA((2,))],
+        scratch_shapes=[
+            VMEM((shape[0], shape[2], shape[1], shape[3]), jnp.float32),
+            pltpu.SemaphoreType.DMA((2,)),
+        ],
         compiler_params=pltpu.CompilerParams(vmem_limit_bytes=VMEM_LIMIT),
     )(*operands)
 

time: 59.2 us -> 57.7 us (0.975)
  Pallas kernels: 59 us -> 57.5 us
    pallas_call x1, Pallas kernels: 54.6 us -> 53.4 us  [ensemble_call(): pl.pallas_call(functools.partial(ensemble_kernel, n_lat, n_lon, n_ens), o...]
where the time goes in v5:
time: 57.7 us; the launch traced here: 57.5 us
  Pallas kernels  57.5 us (100%)
    pallas_call x1, Pallas kernels, ensemble_call(): pl.pallas_call(functools.partial(ensemble_kernel, n_lat, n_lon, n_ens), o...  53.4 us
    pallas_call x1, Pallas kernels, update_call(): pl.pallas_call(update_kernel, out_shape=jax.ShapeDtypeStruct(shape, jnp.f...  4.02 us

profile of v5, /device:TPU:0, one launch (start us, length us, event | category | flops | bytes accessed | tf_op | source)
XLA Modules:
  0.0 57.5 jit_solution(16774094527921823085)
XLA Ops:
  0.0 53.4 %shard_map.64 = (f32[2,40,128]{2,1,0:T(8,128)S(1)}, f32[8,2,8,8,128]{4,3,2,1,0:T(8,128)S(1)}, f32[8,2,8,8,128]{4,3,2,1,0:T(8,128)S(1)}) custom-call(f32[2,8,8,8,128]{4,3,2,1,0:T(8,128)} %bitcast.4, f32[8,128]{1,0:T(8,128)} %refs_1_.1, f32[2,8,128]{2,1,0:T(8,128)} %refs_2_.1, s32[2,1,8,16]{3,2,1,0:T(8,128)} %bitcast.5, f32[2,1,8,16]{3,2,1,0:T(8,128)} %bitcast.6, ...), custom_call_target="tpu_custom_call" | custom-call | tf_op jit(solution)/shard_map/pallas_call | solution.py:825
  53.4 4.0 %shard_map.65 = f32[2,64,8,128]{3,2,1,0:T(8,128)} custom-call(f32[2,40,128]{2,1,0:T(8,128)S(1)} %get-tuple-element.8.gx, f32[8,2,8,8,128]{4,3,2,1,0:T(8,128)S(1)} %get-tuple-element.9.own, f32[8,2,8,8,128]{4,3,2,1,0:T(8,128)S(1)} %get-tuple-element.10.other), custom_call_target="tpu_custom_call" | custom-call | tf_op jit(solution)/shard_map/pallas_call | solution.py:848

commit v6 on v5

--- a/solution.py
+++ b/solution.py
@@ -571,7 +571,6 @@
             if t == 0 and k == 0:
                 for i in range(1, blocks):
                     line_copy(i).start()
-        swap.start()
         for k in range(groups_here):
             got[k, :, :, pl.ds(lat, 1)] = own[pl.ds(lat * groups_here + k, 1)].reshape(
                 2, rows, 1, SUB, cols
@@ -657,6 +656,7 @@
             return carry
 
         lax.fori_loop(0, groups_here, group, 0)
+        swap.start()
         for j in range(share):
             arrived[j, pl.ds(here, 1)] = outgoing[pl.ds(ens * share + j, 1)]
         if t == 0:

time: 57.7 us -> 57.7 us (level)
  no operation moved by 1% of the time
where the time goes in v6:
time: 57.7 us; the launch traced here: 57.5 us
  Pallas kernels  57.5 us (100%)
    pallas_call x1, Pallas kernels, ensemble_call(): pl.pallas_call(functools.partial(ensemble_kernel, n_lat, n_lon, n_ens), o...  53.4 us
    pallas_call x1, Pallas kernels, update_call(): pl.pallas_call(update_kernel, out_shape=jax.ShapeDtypeStruct(shape, jnp.f...  4.02 us

profile of v6, /device:TPU:0, one launch (start us, length us, event | category | flops | bytes accessed | tf_op | source)
XLA Modules:
  0.0 57.5 jit_solution(11895326972393538301)
XLA Ops:
  0.0 53.4 %shard_map.64 = (f32[2,40,128]{2,1,0:T(8,128)S(1)}, f32[8,2,8,8,128]{4,3,2,1,0:T(8,128)S(1)}, f32[8,2,8,8,128]{4,3,2,1,0:T(8,128)S(1)}) custom-call(f32[2,8,8,8,128]{4,3,2,1,0:T(8,128)} %bitcast.4, f32[8,128]{1,0:T(8,128)} %refs_1_.1, f32[2,8,128]{2,1,0:T(8,128)} %refs_2_.1, s32[2,1,8,16]{3,2,1,0:T(8,128)} %bitcast.5, f32[2,1,8,16]{3,2,1,0:T(8,128)} %bitcast.6, ...), custom_call_target="tpu_custom_call" | custom-call | tf_op jit(solution)/shard_map/pallas_call | solution.py:825
  53.4 4.0 %shard_map.65 = f32[2,64,8,128]{3,2,1,0:T(8,128)} custom-call(f32[2,40,128]{2,1,0:T(8,128)S(1)} %get-tuple-element.8.gx, f32[8,2,8,8,128]{4,3,2,1,0:T(8,128)S(1)} %get-tuple-element.9.own, f32[8,2,8,8,128]{4,3,2,1,0:T(8,128)S(1)} %get-tuple-element.10.other), custom_call_target="tpu_custom_call" | custom-call | tf_op jit(solution)/shard_map/pallas_call | solution.py:848
